TPU v7x, 16 devices: a whole 2x2x2 slice. The times are simulated.
16 devices in a mesh: data: 2 (over z), expert: 8 (over y, x, core).
Axes of the slice: x: 2, y: 2, z: 2, core: 2. Of those that a mesh axis runs over, the one named last changes fastest.
Arguments:
- dy: bfloat16 [32768, 768], P(('data', 'expert'))
- gates: float32 [32768, 1], P(('data', 'expert'))
- topk_idx: int32 [32768, 1], P(('data', 'expert'))
- slot: int32 [32768, 1], P(('data', 'expert'))
- yd: bfloat16 [32768, 1, 768], P(('data', 'expert'))
- xd: bfloat16 [16, 2560, 768], P(('data', 'expert'))
- h1: bfloat16 [16, 2560, 3072], P(('data', 'expert'))
- h3: bfloat16 [16, 2560, 3072], P(('data', 'expert'))
- w1: bfloat16 [8, 768, 3072], P('expert')
- w3: bfloat16 [8, 768, 3072], P('expert')
- w2: bfloat16 [8, 3072, 768], P('expert')
Outputs:
- output 1: bfloat16 [32768, 768], P(('data', 'expert'))
- output 2: float32 [32768, 1], P(('data', 'expert'))
- output 3: float32 [8, 768, 3072], P('expert', None, 'data')
- output 4: float32 [8, 768, 3072], P('expert', None, 'data')
- output 5: float32 [8, 3072, 768], P('expert', 'data')
All inputs are finite; a program needn't handle non-finite values.
Results may differ from a plain program's by a relative error of at most 0.0106822.
Values are sent between devices in bfloat16 or wider.
A program may use at most 1 GiB of HBM per device.

v0:
```python
import jax
import jax.numpy as jnp
from jax import lax
from jax.experimental import pallas as pl
from jax.experimental.pallas import tpu as pltpu
from jax.sharding import PartitionSpec as P


F32 = jnp.float32
BF16 = jnp.bfloat16
I32 = jnp.int32


TILE = 64
BT = 4
FC = 768
VMEM_LIMIT = 62 * 1024 * 1024

ANY = pl.BlockSpec(memory_space=pl.ANY)
HBM = pl.BlockSpec(memory_space=pltpu.HBM)
SMEM = pl.BlockSpec(memory_space=pltpu.SMEM)


def _params(**kw):
    return pltpu.CompilerParams(vmem_limit_bytes=VMEM_LIMIT, **kw)


def _cost(flops, nbytes):
    return pl.CostEstimate(flops=int(flops), bytes_accessed=int(nbytes), transcendentals=0)


def _dot(a, b):
    return jnp.dot(a, b, preferred_element_type=F32)


def _dot_nt(a, b):
    return lax.dot_general(a, b, (((1,), (1,)), ((), ())), preferred_element_type=F32)


def _grads(da, h1, h3):
    h1f = h1.astype(F32)
    h3f = h3.astype(F32)
    da = da.astype(BF16).astype(F32)
    s = jax.nn.sigmoid(h1f)
    silu = h1f * s
    a = (silu * h3f).astype(BF16)
    dh1 = ((da * h3f) * (s + silu * (1.0 - s))).astype(BF16)
    dh3 = (da * silu).astype(BF16)
    return a, dh1, dh3


def _scatter_rows(topk, slot, gates, dy, me, ks, cap):
    t, d = dy.shape
    k = len(ks)

    def kernel(meta_ref, e_ref, s_ref, g_ref, dy_ref, *refs):
        outs, v_ref, ob, sem = refs[:k], refs[k], refs[k + 1], refs[k + 2]
        v_ref[...] = (g_ref[...] * dy_ref[...].astype(F32)).astype(BF16)

        @pl.loop(0, k)
        def _(q):
            kq = sum(jnp.where(q == p, ks[p], 0) for p in range(k))
            pos = jnp.where(e_ref[...] == lax.bitwise_xor(kq, meta_ref[1]), s_ref[...], -1)
            row = lax.broadcasted_iota(I32, (cap, t), 0)
            oh = jnp.where(pos == row, 1.0, 0.0).astype(BF16)
            ob[q] = _dot(oh, v_ref[...]).astype(BF16)
            for p in range(k):
                @pl.when(q == p)
                def _():
                    pltpu.make_async_copy(ob.at[p], outs[p], sem.at[p]).start()

        for p in range(k):
            pltpu.make_async_copy(ob.at[p], outs[p], sem.at[p]).wait()

    vm = pl.BlockSpec(memory_space=pltpu.VMEM)
    return pl.pallas_call(
        kernel, in_specs=[SMEM] + [vm] * 4, out_specs=[HBM] * k,
        out_shape=[jax.ShapeDtypeStruct((cap, d), BF16)] * k,
        scratch_shapes=[pltpu.VMEM((t, d), BF16), pltpu.VMEM((k, cap, d), BF16), pltpu.SemaphoreType.DMA((k,))],
        compiler_params=_params(), name="scatter_rows",
        cost_estimate=_cost(2 * k * cap * t * d, 2 * k * cap * d * 2),
    )(me, topk, slot, gates, dy)


def _gather_rows(pos, parts):
    t = pos.shape[0]
    k = len(parts)
    r, d = parts[0].shape
    tb = 512

    def kernel(pos_ref, *refs):
        ins, o_ref, src, sem = refs[:k], refs[k], refs[k + 1], refs[k + 2]

        @pl.when(pl.program_id(0) == 0)
        def _():
            for q in range(k):
                pltpu.make_async_copy(ins[q], src.at[pl.ds(q * r, r)], sem.at[q]).start()
            for q in range(k):
                pltpu.make_async_copy(ins[q], src.at[pl.ds(q * r, r)], sem.at[q]).wait()

        col = lax.broadcasted_iota(I32, (tb, k * r), 1)
        oh = jnp.where(pos_ref[...] == col, 1.0, 0.0).astype(BF16)
        o_ref[...] = _dot(oh, src[...]).astype(BF16)

    return pl.pallas_call(
        kernel, grid=(t // tb,),
        in_specs=[pl.BlockSpec((tb, 1), lambda i: (i, 0))] + [HBM] * k,
        out_specs=pl.BlockSpec((tb, d), lambda i: (i, 0)),
        out_shape=jax.ShapeDtypeStruct((t, d), BF16),
        scratch_shapes=[pltpu.VMEM((k * r, d), BF16), pltpu.SemaphoreType.DMA((k,))],
        compiler_params=_params(), name="gather_rows",
        cost_estimate=_cost(2 * k * r * t * d, 2 * k * r * d * 2),
    )(pos, *parts)


def _own_rows(rng, tl, meta, first, gs, h1, h3, w1, w3, w2, halves, nblk, at):
    ng = len(gs)
    cap, d = gs[0].shape
    _, tile, f = h1.shape
    tps = cap // tile
    fh = f // 2
    rows = BT * tile
    fc = 512
    nc = f // fc
    alias = halves is not None

    def kernel(rng_ref, tl_ref, meta_ref, *refs):
        g_refs, refs = refs[:ng], refs[ng:]
        h1_ref, h3_ref, w1_hbm, w3_hbm, w2_hbm = refs[:5]
        refs = refs[5 + (3 if alias else 0):]
        dxd_refs, refs = refs[:ng], refs[ng:]
        (a_ref, dh1_ref, dh3_ref, w13v, w2v, gall, h1b, h3b, oall, hb, acc,
         wsem, gsem, isem, osem, hsem) = refs
        b0, b1 = rng_ref[at[0]], rng_ref[at[1]]
        half, me = meta_ref[0], meta_ref[1]
        c0 = half * (nc // 2)

        def src_tile(t):
            return lax.bitwise_xor(t // tps, me) * tps + lax.rem(t, tps)

        def tile_copies(b, slot, j):
            t = src_tile(tl_ref[b * BT + j])
            rs = pl.ds(j * tile, tile)
            return (pltpu.make_async_copy(h1_ref.at[t], h1b.at[slot, rs], isem.at[slot, 0, j]),
                    pltpu.make_async_copy(h3_ref.at[t], h3b.at[slot, rs], isem.at[slot, 1, j]))

        def fetch(b, slot):
            for j in range(BT):
                @pl.when(tl_ref[b * BT + j] >= 0)
                def _():
                    for c in tile_copies(b, slot, j):
                        c.start()

                @pl.when(tl_ref[b * BT + j] < 0)
                def _():
                    rs = pl.ds(j * tile, tile)
                    h1b[slot, rs] = jnp.zeros((tile, f), BF16)
                    h3b[slot, rs] = jnp.zeros((tile, f), BF16)

        def arrive(b, slot):
            for j in range(BT):
                @pl.when(tl_ref[b * BT + j] >= 0)
                def _():
                    for c in tile_copies(b, slot, j):
                        c.wait()

        def half_copies(b):
            rs = pl.ds(pl.multiple_of(b * rows, rows), rows)
            return [pltpu.make_async_copy(hb.at[q], r.at[rs], hsem.at[q])
                    for q, r in enumerate((a_ref, dh1_ref, dh3_ref))]

        gcopies = [pltpu.make_async_copy(g_refs[q], gall.at[pl.ds(q * cap, cap)], gsem.at[q]) for q in range(ng)]

        def wcopies(i, parts=(0, 1, 2)):
            c = lax.rem(c0 + i, nc)
            cs = pl.ds(pl.multiple_of(c * fc, fc), fc)
            return [pltpu.make_async_copy(w2_hbm.at[cs], w2v.at[cs], wsem.at[i, 0]) if q == 0 else
                    pltpu.make_async_copy((w1_hbm, w3_hbm)[q - 1].at[:, cs], w13v.at[c, :, pl.ds((q - 1) * fc, fc)],
                                          wsem.at[i, q])
                    for q in parts]

        for c in gcopies + wcopies(0, (0,)):
            c.start()

        @pl.when(b0 < b1)
        def _():
            fetch(b0, 0)

        for c in wcopies(0, (1, 2)):
            c.start()
        for i in range(1, nc):
            for c in wcopies(i):
                c.start()
        oall[...] = jnp.zeros(oall.shape, BF16)
        for c in gcopies:
            c.wait()

        def weights(b, i, part):
            @pl.when(b == b0)
            def _():
                for c in wcopies(i, part):
                    c.wait()

        @pl.loop(b0, b1)
        def _(b):
            slot = lax.rem(b - b0, 2)

            @pl.when(b + 1 < b1)
            def _():
                fetch(b + 1, 1 - slot)

            g = jnp.concatenate(
                [jnp.where(tl_ref[b * BT + j] >= 0,
                           gall[pl.ds(pl.multiple_of(jnp.maximum(tl_ref[b * BT + j] - first * tps, 0) * tile, tile), tile)],
                           jnp.zeros((tile, d), BF16)) for j in range(BT)], axis=0)
            arrive(b, slot)

            @pl.when(b > b0)
            def _():
                for c in half_copies(b - 1):
                    c.wait()

            def col(i):
                c = lax.rem(c0 + i, nc)
                return c, pl.ds(pl.multiple_of(c * fc, fc), fc)

            weights(b, 0, (0,))
            da = _dot_nt(g, w2v[col(0)[1], :])
            for i in range(nc):
                c, cs = col(i)
                weights(b, i, (1, 2))
                if i + 1 < nc:
                    weights(b, i + 1, (0,))
                nxt = _dot_nt(g, w2v[col(i + 1)[1], :]) if i + 1 < nc else None
                a, dh1, dh3 = _grads(da, h1b[slot, :, cs], h3b[slot, :, cs])
                if i < nc // 2:
                    hs = pl.ds(i * fc, fc)
                    hb[0, :, hs] = a
                    hb[1, :, hs] = dh1
                    hb[2, :, hs] = dh3
                y = _dot_nt(jnp.concatenate([dh1, dh3], axis=1), w13v[c])
                if i == 0:
                    acc[...] = y
                else:
                    acc[...] += y
                da = nxt
                if i == nc // 2 - 1:
                    for cp in half_copies(b):
                        cp.start()
            for j in range(BT):
                @pl.when(tl_ref[b * BT + j] >= 0)
                def _():
                    t = tl_ref[b * BT + j] - first * tps
                    oall[pl.ds(pl.multiple_of(t * tile, tile), tile)] = acc[pl.ds(j * tile, tile)].astype(BF16)

        @pl.when(b0 >= b1)
        def _():
            for i in range(nc):
                for c in wcopies(i):
                    c.wait()

        outs = [pltpu.make_async_copy(oall.at[pl.ds(q * cap, cap)], dxd_refs[q], osem.at[q]) for q in range(ng)]
        for c in outs:
            c.start()

        @pl.when(b0 < b1)
        def _():
            for c in half_copies(b1 - 1):
                c.wait()

        if alias:
            @pl.when(lax.rem(b1, 2) == 1)
            def _():
                hb[...] = jnp.zeros(hb.shape, BF16)
                for c in half_copies(b1):
                    c.start()
                for c in half_copies(b1):
                    c.wait()
        for c in outs:
            c.wait()

    hshape = jax.ShapeDtypeStruct((nblk * rows, fh), BF16)
    base = 3 + ng + 5
    return pl.pallas_call(
        kernel, in_specs=[SMEM] * 3 + [HBM] * (ng + 5 + (3 if alias else 0)), out_specs=[HBM] * (ng + 3),
        out_shape=[jax.ShapeDtypeStruct((cap, d), BF16)] * ng + [hshape] * 3,
        input_output_aliases={base + q: ng + q for q in range(3)} if alias else {},
        scratch_shapes=[pltpu.VMEM((nc, d, 2 * fc), BF16), pltpu.VMEM((f, d), BF16),
                        pltpu.VMEM((ng * cap, d), BF16), pltpu.VMEM((2, rows, f), BF16), pltpu.VMEM((2, rows, f), BF16),
                        pltpu.VMEM((ng * cap, d), BF16), pltpu.VMEM((3, rows, fh), BF16),
                        pltpu.VMEM((rows, d), F32),
                        pltpu.SemaphoreType.DMA((nc, 3)), pltpu.SemaphoreType.DMA((ng,)),
                        pltpu.SemaphoreType.DMA((2, 2, BT)), pltpu.SemaphoreType.DMA((ng,)),
                        pltpu.SemaphoreType.DMA((3,))],
        compiler_params=_params(), name="own_rows",
        cost_estimate=_cost(2 * 200 * ng * d * f * 3, 5e7),
    )(rng, tl, meta, *gs, h1, h3, w1, w3, w2, *(halves if alias else ()))


def _plan(occ, occo, meta, cut, tps, size):
    nt = occ.shape[0]

    def kernel(occ_ref, occo_ref, meta_ref, tl_ref, tlo_ref, bnd_ref):
        me = meta_ref[1]
        for li, (o_ref, t_ref) in enumerate(((occ_ref, tl_ref), (occo_ref, tlo_ref))):
            pos = jnp.int32(0)
            bnd_ref[li * 4] = pos
            for part, (lo, hi) in enumerate(((0, cut * tps), (cut * tps, nt))):
                def step(t, pos):
                    t_ref[pos] = t
                    return pos + o_ref[lax.bitwise_xor(t // tps, me) * tps + lax.rem(t, tps)]

                pos = lax.fori_loop(lo, hi, step, pos)
                end = ((pos + BT - 1) // BT) * BT

                def pad(i, c):
                    t_ref[i] = -1
                    return c

                lax.fori_loop(pos, end if part == 0 else end + BT, pad, 0)
                pos = end
                bnd_ref[li * 4 + 1 + part] = pos // BT
            bnd_ref[li * 4 + 3] = (pos // BT + 1) // 2

    return pl.pallas_call(
        kernel, in_specs=[SMEM] * 3, out_specs=[SMEM] * 3,
        out_shape=[jax.ShapeDtypeStruct((size,), I32), jax.ShapeDtypeStruct((size,), I32), jax.ShapeDtypeStruct((8,), I32)],
        name="plan", cost_estimate=_cost(1e6, 1e3))(occ, occo, meta)


def _dw(rng, tl, meta, first, gs, x, own, peer, sums, at, bt):
    ng = len(gs)
    cap, d = gs[0].shape
    _, tile, _ = x.shape
    tps = cap // tile
    fh = own[0].shape[1] if own else peer[0].shape[1] // 2
    rows = bt * tile
    fc = FC
    nc = fh // fc
    nadd = 3 if sums else 0
    mb = -(-ng * tps // bt) + (1 if own else 0)

    def kernel(rng_ref, tl_ref, meta_ref, *refs):
        g_refs, x_ref, refs = refs[:ng], refs[ng], refs[ng + 1:]
        s_refs, q_refs, o_refs = refs[:3], refs[3:3 + nadd], refs[3 + nadd:6 + nadd]
        (gall, xb, xt, gb, sv, p1, p3, p2, gsem, xsem, ssem, psem, osem) = refs[6 + nadd:]
        b0, b1 = rng_ref[at[0]], rng_ref[at[1]]
        half, me = meta_ref[0], meta_ref[1]

        def xcopy(b, j):
            t = tl_ref[b * bt + j]
            t = lax.bitwise_xor(t // tps, me) * tps + lax.rem(t, tps) if own else t - first * tps
            return pltpu.make_async_copy(x_ref.at[t], xb.at[b - b0, pl.ds(j * tile, tile)], xsem.at[b - b0, j])

        gcopies = [pltpu.make_async_copy(g_refs[q], gall.at[pl.ds(q * cap, cap)], gsem.at[q]) for q in range(ng)]

        def pcopies(c, slot):
            cs = pl.ds(pl.multiple_of(c * fc, fc), fc)
            views = ((p1, (slice(None), cs)), (p3, (slice(None), cs)), (p2, (cs, slice(None))))
            return [pltpu.make_async_copy(q.at[ix], p.at[slot], psem.at[slot, r])
                    for r, (q, (p, ix)) in enumerate(zip(q_refs, views))]

        def ocopies(c, slot):
            cs = pl.ds(pl.multiple_of(c * fc, fc), fc)
            views = ((p1, (slice(None), cs)), (p3, (slice(None), cs)), (p2, (cs, slice(None))))
            return [pltpu.make_async_copy(p.at[slot], o.at[ix], osem.at[slot, r])
                    for r, (o, (p, ix)) in enumerate(zip(o_refs, views))]

        def wcopies(c, slot):
            cs = pl.ds(pl.multiple_of(half * fh + c * fc, fc), fc)
            return [pltpu.make_async_copy(s.at[:, cs] if r < 2 else s.at[cs], sv.at[slot, r], ssem.at[slot, r])
                    for r, s in enumerate(s_refs)]

        def scopies(c, b, slot):
            rs = pl.ds(pl.multiple_of(b * rows, rows), rows)
            cs = pl.ds(pl.multiple_of(c * fc, fc), fc)
            return [pltpu.make_async_copy(s.at[rs, cs], sv.at[slot, r], ssem.at[slot, r]) for r, s in enumerate(s_refs)]

        for c in gcopies:
            c.start()

        @pl.loop(b0, b1)
        def _(b):
            for j in range(bt):
                @pl.when(tl_ref[b * bt + j] >= 0)
                def _():
                    xcopy(b, j).start()

                @pl.when(tl_ref[b * bt + j] < 0)
                def _():
                    xb[b - b0, pl.ds(j * tile, tile)] = jnp.zeros((tile, d), BF16)

        if peer:
            for cp in wcopies(0, 0):
                cp.start()
        if sums:
            for cp in pcopies(0, 0):
                cp.start()
        if own:
            @pl.when(b0 < b1)
            def _():
                for cp in scopies(0, b0, 0):
                    cp.start()
        for c in gcopies:
            c.wait()

        @pl.loop(b0, b1)
        def _(b):
            for j in range(bt):
                @pl.when(tl_ref[b * bt + j] >= 0)
                def _():
                    xcopy(b, j).wait()
                    t = tl_ref[b * bt + j] - first * tps
                    gb[b - b0, pl.ds(j * tile, tile)] = gall[pl.ds(pl.multiple_of(t * tile, tile), tile)]

                @pl.when(tl_ref[b * bt + j] < 0)
                def _():
                    gb[b - b0, pl.ds(j * tile, tile)] = jnp.zeros((tile, d), BF16)
            xt[b - b0] = xb[b - b0].T

        @pl.loop(0, nc)
        def _(c):
            ps = lax.rem(c, 2)
            if peer:
                @pl.when(c + 1 < nc)
                def _():
                    for cp in wcopies(c + 1, 1 - ps):
                        cp.start()

                for cp in wcopies(c, ps):
                    cp.wait()

            if sums:
                @pl.when(c + 1 < nc)
                def _():
                    @pl.when(c >= 1)
                    def _():
                        for cp in ocopies(c - 1, 1 - ps):
                            cp.wait()

                    for cp in pcopies(c + 1, 1 - ps):
                        cp.start()

                for cp in pcopies(c, ps):
                    cp.wait()
            else:
                @pl.when(c >= 2)
                def _():
                    for cp in ocopies(c - 2, ps):
                        cp.wait()

                p1[ps] = jnp.zeros((d, fc), F32)
                p3[ps] = jnp.zeros((d, fc), F32)
                p2[ps] = jnp.zeros((fc, d), F32)

            @pl.loop(b0, b1)
            def _(b):
                i = b - b0
                if own:
                    slot = lax.rem(c * (b1 - b0) + i, 2)

                    @pl.when(b + 1 < b1)
                    def _():
                        for cp in scopies(c, b + 1, 1 - slot):
                            cp.start()

                    @pl.when((b + 1 == b1) & (c + 1 < nc))
                    def _():
                        for cp in scopies(c + 1, b0, 1 - slot):
                            cp.start()

                    for cp in scopies(c, b, slot):
                        cp.wait()
                    a, dh1, dh3 = sv[slot, 0], sv[slot, 1], sv[slot, 2]
                else:
                    h1 = _dot(xb[i], sv[ps, 0]).astype(BF16)
                    h3 = _dot(xb[i], sv[ps, 1]).astype(BF16)
                    da = _dot_nt(gb[i], sv[ps, 2])
                    a, dh1, dh3 = _grads(da, h1, h3)
                p1[ps] += _dot(xt[i], dh1)
                p3[ps] += _dot(xt[i], dh3)
                p2[ps] += _dot(a.T, gb[i])

            for cp in ocopies(c, ps):
                cp.start()

        for c in (nc - 2, nc - 1):
            for cp in ocopies(c, c % 2):
                cp.wait()

    srows = rows if own else d
    outs = [jax.ShapeDtypeStruct((d, fh), F32), jax.ShapeDtypeStruct((d, fh), F32), jax.ShapeDtypeStruct((fh, d), F32)]
    return pl.pallas_call(
        kernel, in_specs=[SMEM] * 3 + [HBM] * (ng + 4 + nadd), out_specs=[HBM] * 3, out_shape=outs,
        scratch_shapes=[pltpu.VMEM((ng * cap, d), BF16), pltpu.VMEM((mb, rows, d), BF16), pltpu.VMEM((mb, d, rows), BF16),
                        pltpu.VMEM((mb, rows, d), BF16), pltpu.VMEM((2, 3, srows, fc), BF16),
                        pltpu.VMEM((2, d, fc), F32), pltpu.VMEM((2, d, fc), F32), pltpu.VMEM((2, fc, d), F32),
                        pltpu.SemaphoreType.DMA((ng,)), pltpu.SemaphoreType.DMA((mb, bt)),
                        pltpu.SemaphoreType.DMA((2, 3)), pltpu.SemaphoreType.DMA((2, 3)), pltpu.SemaphoreType.DMA((2, 3))],
        compiler_params=_params(), name="own_dw" if own else "peer_dw",
        cost_estimate=_cost(2 * 200 * ng * d * fh * (3 if own else 6), 5e7),
    )(rng, tl, meta, *gs, x, *(own or peer), *(sums or ()))


def solution(mesh):
    ne = mesh.shape['expert']
    nd = mesh.shape['data']
    tok = P(('data', 'expert'), None)
    buf = P(('data', 'expert'), None, None)
    wsp = P('expert', None, None)
    zswap = [(i, nd - 1 - i) for i in range(nd)]
    ka = ne * 3 // 4
    groups = ((2, 4, 3, 5), (6, 7, 1, 0))

    def run(dy, gates, topk_idx, slot, yd, xd, h1, h3, w1, w3, w2):
        t, d = dy.shape
        cap = xd.shape[1] // ne
        f = w1.shape[2]
        nt = xd.shape[1] // TILE
        tps = cap // TILE
        me = lax.axis_index('expert').astype(I32)
        grp = lax.axis_index('data').astype(I32)
        meta = jnp.stack([grp, me])
        xor = lambda k: [(i, i ^ k) for i in range(ne)]
        swap = lambda v: lax.ppermute(v, 'data', zswap)

        x4 = xd.reshape(nt, TILE, d)
        x8 = xd.reshape(ne, cap, d)
        xk = [lax.dynamic_index_in_dim(x8, me ^ k, 0, keepdims=True) for k in range(ne)]
        xo = [swap(jnp.concatenate(xk[i:j], axis=0).reshape((j - i) * tps, TILE, d)) for i, j in ((0, ka), (ka, ne))]

        send = [None] * ne
        for ks in groups:
            for k, v in zip(ks, _scatter_rows(topk_idx.reshape(1, t), slot.reshape(1, t), gates, dy, meta, ks, cap)):
                send[k] = v
        dyd = [send[0]]
        for k in range(1, ne):
            dyd.append(lax.ppermute(send[k], 'expert', xor(k)))
        dyo = []
        for k in range(ne):
            dyo.append(swap(dyd[k]))

        occ = jnp.any(x4 != 0, axis=(1, 2)).astype(I32)
        occo = swap(occ)
        nblk = -(-ka * tps // BT) + -(-(ne - ka) * tps // BT) + 1
        tl, tlo, bnd = _plan(occ, occo, meta, ka, tps, (nblk + 1) * BT)

        h14, h34 = h1.reshape(nt, TILE, f), h3.reshape(nt, TILE, f)
        wts = (w1[0], w3[0], w2[0])
        *da, ha, hd1, hd3 = _own_rows(bnd, tl, meta, 0, dyd[:ka], h14, h34, *wts, None, nblk, (0, 1))
        back = [da[0]]
        for k in range(1, ka):
            back.append(lax.ppermute(da[k], 'expert', xor(k)))
        *db, ha, hd1, hd3 = _own_rows(bnd, tl, meta, ka, dyd[ka:], h14, h34, *wts, (ha, hd1, hd3), nblk, (1, 2))
        for k in range(ka, ne):
            back.append(lax.ppermute(db[k - ka], 'expert', xor(k)))
        sums = _dw(bnd, tl, meta, 0, dyd, x4, (ha, hd1, hd3), None, None, (0, 3), 2 * BT)
        dg = jnp.einsum('tkd,td->tk', yd, dy, preferred_element_type=F32)
        cpos = jnp.where(slot >= 0, (topk_idx ^ me) * cap + slot, -1)
        dx = _gather_rows(cpos, back)
        sums = _dw(bnd, tlo, meta, 0, dyo[:ka], xo[0], None, wts, sums, (4, 5), BT)
        sums = _dw(bnd, tlo, meta, ka, dyo[ka:], xo[1], None, wts, sums, (5, 6), BT)
        dw1, dw3, dw2 = sums
        return dx, dg, dw1[None], dw3[None], dw2[None]


    return jax.shard_map(run, mesh=mesh,
                         in_specs=(tok, tok, tok, tok, buf, buf, buf, buf, wsp, wsp, wsp),
                         out_specs=(tok, tok, P('expert', None, 'data'), P('expert', None, 'data'), P('expert', 'data', None)),
                         check_vma=False)
```

profile of v0, /device:TPU:14, one launch (start us, length us, event | category | flops | bytes accessed | tf_op | source)
XLA Modules:
  0.0 283.7 jit_solution(2586260514714638863)
XLA Ops:
  0.6 2.0 copy.38.g_ref
  2.7 0.7 pad_add_fusion.meta_ref
  3.3 8.4 %scatter_rows.2 = (bf16[320,768]{1,0:T(8,128)(2,1)}, bf16[320,768]{1,0:T(8,128)(2,1)}, bf16[320,768]{1,0:T(8,128)(2,1)}, bf16[320,768]{1,0:T(8,128)(2,1)}) custom-call(s32[2]{0:T(128)} %pad_add_fusion.meta_ref, s32[1,2048]{1,0:T(1,128)} %bitcast.45, s32[1,2048]{1,0:T(1,128)} %bitcast.43, f32[2048,1]{1,0:T(8,128)} %copy.38.g_ref, bf16[2048,768]{1,0:T(8,128)(2,1)} %dy_ref.3), custom_call_target="tpu_custom_call" | custom-call | flops 4026531840 | bytes 3932160 | tf_op jit(solution)/shard_map/scatter_rows/pallas_call | solution.py:76
  11.7 0.0 collective-permute-start.1
  11.8 8.4 %scatter_rows.3 = (bf16[320,768]{1,0:T(8,128)(2,1)}, bf16[320,768]{1,0:T(8,128)(2,1)}, bf16[320,768]{1,0:T(8,128)(2,1)}, bf16[320,768]{1,0:T(8,128)(2,1)}) custom-call(s32[2]{0:T(128)} %pad_add_fusion.meta_ref, s32[1,2048]{1,0:T(1,128)} %bitcast.46, s32[1,2048]{1,0:T(1,128)} %bitcast.44, f32[2048,1]{1,0:T(8,128)} %copy.38.g_ref, bf16[2048,768]{1,0:T(8,128)(2,1)} %dy_ref.3), custom_call_target="tpu_custom_call" | custom-call | flops 4026531840 | bytes 3932160 | tf_op jit(solution)/shard_map/scatter_rows/pallas_call | solution.py:76
  20.2 0.0 copy-start.4
  20.2 0.0 copy-start.3
  20.2 0.6 collective-permute-start.2
  20.8 1.3 collective-permute-start.3
  22.1 0.5 collective-permute-start.4
  22.6 3.0 %compare_reduce_fusion = pred[2560]{0:T(1024)(128)(4,1)S(1)} fusion(bf16[1,2560,768]{2,1,0:T(8,128)(2,1)} %param.16), kind=kLoop, calls=%fused_computation | loop fusion | flops 3929600 | bytes 3934720 | tf_op jit(solution)/shard_map/reduce_or | solution.py:543
  25.6 0.1 reduce_or.14
  25.7 0.1 reduce_or.18
  25.9 0.0 copy-start.10
  25.9 0.5 collective-permute-start
  26.4 0.4 copy.33
  26.8 0.1 xor_multiply_fusion
  26.9 1.9 dynamic-slice_dynamic-update-slice_fusion.5
  28.7 1.9 dynamic-slice_dynamic-update-slice_fusion.4
  30.6 1.9 dynamic-slice_dynamic-update-slice_fusion.3
  32.4 1.9 dynamic-slice_dynamic-update-slice_fusion.2
  34.3 1.8 dynamic-slice_dynamic-update-slice_fusion.1
  36.1 2.2 dynamic-slice_dynamic-update-slice_fusion
  38.4 0.0 collective-permute-done.occo_ref
  38.4 0.9 collective-permute-start.5
  39.3 1.0 pad_maximum_fusion
  40.3 0.3 copy.35
  40.6 0.4 copy.37
  41.0 0.5 copy.36
  41.5 4.3 %fusion = f32[2048]{0:T(1024)} fusion(bf16[2048,768]{1,0:T(8,128)(2,1)} %dy_ref.3, bf16[2048,1,768]{2,0,1:T(8,128)(2,1)} %param.15), kind=kLoop, calls=%fused_computation.2 | loop fusion | flops 6289408 | bytes 6299648 | tf_op jit(solution)/shard_map/tkd,td->tk/dot_general | solution.py:558
  45.8 2.7 plan.1
  48.5 0.0 copy-start.5
  48.5 0.8 copy-done.5
  49.3 0.6 collective-permute-start.11
  49.9 2.4 collective-permute-start.12
  52.3 1.6 collective-permute-start.24
  53.9 0.4 collective-permute-start.18
  54.4 34.2 %own_rows.2 = (bf16[320,768]{1,0:T(8,128)(2,1)}, bf16[320,768]{1,0:T(8,128)(2,1)}, bf16[320,768]{1,0:T(8,128)(2,1)}, bf16[320,768]{1,0:T(8,128)(2,1)}, bf16[320,...) custom-call(s32[8]{0:T(128)} %get-tuple-element.39.rng_ref, ...), custom_call_target="tpu_custom_call" | custom-call | flops 16986931200 | bytes 50000000 | tf_op jit(solution)/shard_map/own_rows/pallas_call | solution.py:284
  88.6 0.8 copy-done.2
  89.3 16.5 %own_rows.3 = (bf16[320,768]{1,0:T(8,128)(2,1)}, bf16[320,768]{1,0:T(8,128)(2,1)}, bf16[3072,1536]{1,0:T(8,128)(2,1)}, bf16[3072,1536]{1,0:T(8,128)(2,1)}, bf16[3072,1536]{1,0:T(8,128)(2,1)}) custom-call(s32[8]{0:T(128)} %get-tuple-element.39.rng_ref, s32[52]{0:T(128)} %get-tuple-element.40.tl_ref, ...), custom_call_target="tpu_custom_call", output_to_operand_aliasing={{2}: (10, {}), {3}: (11, {}), {4}: (12, {})} | custom-call | flops 5662310400 | bytes 50000000 | tf_op jit(solution)/shard_map/own_rows/pallas_call | solution.py:284
  105.9 5.2 %collective-permute-start.13 = (bf16[320,768]{1,0:T(8,128)(2,1)}, bf16[320,768]{1,0:T(8,128)(2,1)}, u32[]{:S(2)}, u32[]{:S(2)}) collective-permute-start(bf16[320,768]{1,0:T(8,128)(2,1)} %get-tuple-element.58), channel_id=1, source_target_pairs={{0,6},{1,7},{2,4},{3,5},{4,2},{5,3},{6,0},{7,1},{8,14},{9,15},{10,... | collective-permute-start | bytes 1474568 | tf_op jit(solution)/shard_map/ppermute | solution.py:556
  111.1 17.9 %collective-permute-done.18.refs_0_ = bf16[320,768]{1,0:T(8,128)(2,1)} collective-permute-done((bf16[320,768]{1,0:T(8,128)(2,1)}, bf16[320,768]{1,0:T(8,128)(2,1)}, u32[]{:S(2)}, u32[]{:S(2)}) %collective-permute-start.18) | collective-permute-done | bytes 491552 | tf_op jit(solution)/shard_map/ppermute | solution.py:525
  129.0 1.6 collective-permute-start.19
  130.6 1.1 broadcast_select_fusion.pos_ref
  131.7 9.9 %collective-permute-done.19.refs_1_ = bf16[320,768]{1,0:T(8,128)(2,1)} collective-permute-done((bf16[320,768]{1,0:T(8,128)(2,1)}, bf16[320,768]{1,0:T(8,128)(2,1)}, u32[]{:S(2)}, u32[]{:S(2)}) %collective-permute-start.19) | collective-permute-done | bytes 491552 | tf_op jit(solution)/shard_map/ppermute | solution.py:525
  141.6 0.6 collective-permute-start.7
  142.2 1.3 collective-permute-start.8
  143.5 0.8 collective-permute-start.9
  144.3 26.9 %own_dw.1 = (f32[768,1536]{1,0:T(8,128)}, f32[768,1536]{1,0:T(8,128)}, f32[1536,768]{1,0:T(8,128)}) custom-call(s32[8]{0:T(128)} %get-tuple-element.39.rng_ref, s32[52]{0:T(128)} %get-tuple-element.40.tl_ref, s32[2]{0:T(128)} %pad_add_fusion.meta_ref, bf16[320,768]{1,0:T(8,128)(2,1)} %get-tuple-element.41.refs_0_, bf16[320,768]{1,0:T(8,128)(2,1)} %copy-done.5, ...), custom_call_target="tpu_custom_call" | custom-call | flops 11324620800 | bytes 50000000 | tf_op jit(solution)/shard_map/own_dw/pallas_call | solution.py:493
  171.2 5.0 %collective-permute-start.20 = (bf16[320,768]{1,0:T(8,128)(2,1)}, bf16[320,768]{1,0:T(8,128)(2,1)S(1)}, u32[]{:S(2)}, u32[]{:S(2)}) collective-permute-start(bf16[320,768]{1,0:T(8,128)(2,1)} %collective-permute-done.2.refs_2_), channel_id=1, source_target_pairs={{0,8},{8,0},{1,9},{9,1},{2,10},{10,2},{3,11},{11,3},{4,12},{12,4},... | collective-permute-start | bytes 1474568 | tf_op jit(solution)/shard_map/ppermute | solution.py:525
  176.2 0.1 collective-permute-start.21
  176.3 2.0 collective-permute-start.22
  178.2 0.1 collective-permute-start.23
  178.3 13.1 %gather_rows.1 = bf16[2048,768]{1,0:T(8,128)(2,1)} custom-call(s32[2048,1]{1,0:T(8,128)} %broadcast_select_fusion.pos_ref, bf16[320,768]{1,0:T(8,128)(2,1)} %get-tuple-element.47.refs_0_, bf16[320,768]{1,0:T(8,128)(2,1)} %copy-done.7, bf16[320,768]{1,0:T(8,128)(2,1)} %copy-done.8, bf16[320,768]{1,0:T(8,128)(2,1)} %copy-done.9, ...), custom_call_target="tpu_custom_call" | custom-call | flops 8053063680 | bytes 7864320 | tf_op jit(solution)/shard_map/gather_rows/pallas_call | solution.py:105
  191.5 0.8 copy-done.6
  192.3 2.0 collective-permute-start.17
  194.3 4.9 %collective-permute-done.21.refs_3_ = bf16[320,768]{1,0:T(8,128)(2,1)} collective-permute-done((bf16[320,768]{1,0:T(8,128)(2,1)}, bf16[320,768]{1,0:T(8,128)(2,1)}, u32[]{:S(2)}, u32[]{:S(2)}) %collective-permute-start.21) | collective-permute-done | bytes 491552 | tf_op jit(solution)/shard_map/ppermute | solution.py:525
  199.1 2.0 collective-permute-start.15
  201.1 8.5 %collective-permute-done.22.refs_4_ = bf16[320,768]{1,0:T(8,128)(2,1)} collective-permute-done((bf16[320,768]{1,0:T(8,128)(2,1)}, bf16[320,768]{1,0:T(8,128)(2,1)}, u32[]{:S(2)}, u32[]{:S(2)}) %collective-permute-start.22) | collective-permute-done | bytes 491552 | tf_op jit(solution)/shard_map/ppermute | solution.py:525
  209.7 2.0 collective-permute-start.16
  211.7 8.5 %collective-permute-done.23.refs_5_ = bf16[320,768]{1,0:T(8,128)(2,1)} collective-permute-done((bf16[320,768]{1,0:T(8,128)(2,1)}, bf16[320,768]{1,0:T(8,128)(2,1)}, u32[]{:S(2)}, u32[]{:S(2)}) %collective-permute-start.23) | collective-permute-done | bytes 491552 | tf_op jit(solution)/shard_map/ppermute | solution.py:525
  220.2 32.0 %peer_dw.2 = (f32[768,1536]{1,0:T(8,128)}, f32[768,1536]{1,0:T(8,128)}, f32[1536,768]{1,0:T(8,128)}) custom-call(s32[8]{0:T(128)} %get-tuple-element.39.rng_ref, s32[52]{0:T(128)} %get-tuple-element.60.tl_ref, s32[2]{0:T(128)} %pad_add_fusion.meta_ref, bf16[320,768]{1,0:T(8,128)(2,1)} %collective-permute-done.18.refs_0_, ...), custom_call_target="tpu_custom_call" | custom-call | flops 16986931200 | bytes 50000000 | tf_op jit(solution)/shard_map/peer_dw/pallas_call | solution.py:493
  252.2 9.3 %collective-permute-done.16.refs_1_ = bf16[320,768]{1,0:T(8,128)(2,1)} collective-permute-done((bf16[320,768]{1,0:T(8,128)(2,1)}, bf16[320,768]{1,0:T(8,128)(2,1)}, u32[]{:S(2)}, u32[]{:S(2)}) %collective-permute-start.16) | collective-permute-done | bytes 491552 | tf_op jit(solution)/shard_map/ppermute | solution.py:525
  261.5 22.0 %peer_dw.3 = (f32[768,1536]{1,0:T(8,128)}, f32[768,1536]{1,0:T(8,128)}, f32[1536,768]{1,0:T(8,128)}) custom-call(s32[8]{0:T(128)} %get-tuple-element.39.rng_ref, s32[52]{0:T(128)} %get-tuple-element.60.tl_ref, s32[2]{0:T(128)} %pad_add_fusion.meta_ref, bf16[320,768]{1,0:T(8,128)(2,1)} %collective-permute-done.15.refs_0_, ...), custom_call_target="tpu_custom_call" | custom-call | flops 5662310400 | bytes 50000000 | tf_op jit(solution)/shard_map/peer_dw/pallas_call | solution.py:493
  (41 shorter events, 0.1 us)
Async XLA Ops:
  11.7 36.8 %collective-permute-start.1 = (bf16[320,768]{1,0:T(8,128)(2,1)}, bf16[320,768]{1,0:T(8,128)(2,1)S(1)}, u32[]{:S(2)}, u32[]{:S(2)}) collective-permute-start(bf16[320,768]{1,0:T(8,128)(2,1)} %get-tuple-element.42), channel_id=1, source_target_pairs={{0,1},{1,0},{2,3},{3,2},{4,5},{5,4},{6,7},{7,6},{8,9},{9,8},{10,11... | collective-permute-start | bytes 1474568 | tf_op jit(solution)/shard_map/ppermute | solution.py:538
  20.2 6.2 %copy-start.4 = (s32[2048,1]{0,1:T(1,128)S(1)}, s32[2048,1]{0,1:T(1,128)}, u32[]{:S(2)}) copy-start(s32[2048,1]{0,1:T(1,128)} %param.13) | copy-start | bytes 24580
  20.2 6.5 %copy-start.3 = (s32[2048,1]{0,1:T(1,128)S(1)}, s32[2048,1]{0,1:T(1,128)}, u32[]{:S(2)}) copy-start(s32[2048,1]{0,1:T(1,128)} %param.14) | copy-start | bytes 24580
  20.2 29.7 %collective-permute-start.2 = (bf16[320,768]{1,0:T(8,128)(2,1)}, bf16[320,768]{1,0:T(8,128)(2,1)}, u32[]{:S(2)}, u32[]{:S(2)}) collective-permute-start(bf16[320,768]{1,0:T(8,128)(2,1)} %get-tuple-element.43), channel_id=1, source_target_pairs={{0,2},{1,3},{2,0},{3,1},{4,6},{5,7},{6,4},{7,5},{8,10},{9,11},{10,... | collective-permute-start | bytes 1474568 | tf_op jit(solution)/shard_map/ppermute | solution.py:538
  20.8 31.5 %collective-permute-start.3 = (bf16[320,768]{1,0:T(8,128)(2,1)}, bf16[320,768]{1,0:T(8,128)(2,1)}, u32[]{:S(2)}, u32[]{:S(2)}) collective-permute-start(bf16[320,768]{1,0:T(8,128)(2,1)} %get-tuple-element.44), channel_id=1, source_target_pairs={{0,3},{1,2},{2,1},{3,0},{4,7},{5,6},{6,5},{7,4},{8,11},{9,10},{10,... | collective-permute-start | bytes 1474568 | tf_op jit(solution)/shard_map/ppermute | solution.py:538
  22.1 31.8 %collective-permute-start.4 = (bf16[320,768]{1,0:T(8,128)(2,1)}, bf16[320,768]{1,0:T(8,128)(2,1)}, u32[]{:S(2)}, u32[]{:S(2)}) collective-permute-start(bf16[320,768]{1,0:T(8,128)(2,1)} %get-tuple-element.45), channel_id=1, source_target_pairs={{0,4},{1,5},{2,6},{3,7},{4,0},{5,1},{6,2},{7,3},{8,12},{9,13},{10,... | collective-permute-start | bytes 1474568 | tf_op jit(solution)/shard_map/ppermute | solution.py:538
  25.9 10.3 %copy-start.10 = (s32[40]{0:T(128)}, s32[40]{0:T(128)S(1)}, u32[]{:S(2)}) copy-start(s32[40]{0:T(128)S(1)} %convert_element_type.3.occ_ref) | copy-start | bytes 484
  25.9 12.5 %collective-permute-start = (s32[40]{0:T(128)S(1)}, s32[40]{0:T(128)S(1)}, u32[]{:S(2)}, u32[]{:S(2)}) collective-permute-start(s32[40]{0:T(128)S(1)} %convert_element_type.3.occ_ref), channel_id=1, source_target_pairs={{0,8},{8,0},{1,9},{9,1},{2,10},{10,2},{3,11},{11,3},{4,12},{12,4},... | collective-permute-start | bytes 488 | tf_op jit(solution)/shard_map/ppermute | solution.py:525
  38.4 7.4 %copy-start.11 = (s32[40]{0:T(128)}, s32[40]{0:T(128)S(1)}, u32[]{:S(2)}) copy-start(s32[40]{0:T(128)S(1)} %collective-permute-done.occo_ref) | copy-start | bytes 484
  38.4 16.0 %collective-permute-start.5 = (bf16[320,768]{1,0:T(8,128)(2,1)}, bf16[320,768]{1,0:T(8,128)(2,1)}, u32[]{:S(2)}, u32[]{:S(2)}) collective-permute-start(bf16[320,768]{1,0:T(8,128)(2,1)} %get-tuple-element.46), channel_id=1, source_target_pairs={{0,5},{1,4},{2,7},{3,6},{4,1},{5,0},{6,3},{7,2},{8,13},{9,12},{10,... | collective-permute-start | bytes 1474568 | tf_op jit(solution)/shard_map/ppermute | solution.py:538
  48.5 0.8 copy-start.5
  49.3 39.2 %collective-permute-start.11 = (bf16[320,768]{1,0:T(8,128)(2,1)}, bf16[320,768]{1,0:T(8,128)(2,1)S(1)}, u32[]{:S(2)}, u32[]{:S(2)}) collective-permute-start(bf16[320,768]{1,0:T(8,128)(2,1)} %get-tuple-element.53), channel_id=1, source_target_pairs={{0,6},{1,7},{2,4},{3,5},{4,2},{5,3},{6,0},{7,1},{8,14},{9,15},{10,... | collective-permute-start | bytes 1474568 | tf_op jit(solution)/shard_map/ppermute | solution.py:538
  49.9 38.6 %collective-permute-start.12 = (bf16[320,768]{1,0:T(8,128)(2,1)}, bf16[320,768]{1,0:T(8,128)(2,1)}, u32[]{:S(2)}, u32[]{:S(2)}) collective-permute-start(bf16[320,768]{1,0:T(8,128)(2,1)} %get-tuple-element.54), channel_id=1, source_target_pairs={{0,7},{1,6},{2,5},{3,4},{4,3},{5,2},{6,1},{7,0},{8,15},{9,14},{10,... | collective-permute-start | bytes 1474568 | tf_op jit(solution)/shard_map/ppermute | solution.py:538
  52.3 167.9 %collective-permute-start.24 = (bf16[30,64,768]{2,1,0:T(8,128)(2,1)}, bf16[30,64,768]{2,1,0:T(8,128)(2,1)}, u32[]{:S(2)}, u32[]{:S(2)}) collective-permute-start(bf16[30,64,768]{2,1,0:T(8,128)(2,1)} %bitcast.13), channel_id=1, source_target_pairs={{0,8},{8,0},{1,9},{9,1},{2,10},{10,2},{3,11},{11,3},{4,12},{12,4},... | collective-permute-start | bytes 8847368 | tf_op jit(solution)/shard_map/ppermute | solution.py:525
  53.9 75.1 %collective-permute-start.18 = (bf16[320,768]{1,0:T(8,128)(2,1)}, bf16[320,768]{1,0:T(8,128)(2,1)}, u32[]{:S(2)}, u32[]{:S(2)}) collective-permute-start(bf16[320,768]{1,0:T(8,128)(2,1)} %get-tuple-element.41.refs_0_), channel_id=1, source_target_pairs={{0,8},{8,0},{1,9},{9,1},{2,10},{10,2},{3,11},{11,3},{4,12},{12,4},... | collective-permute-start | bytes 1474568 | tf_op jit(solution)/shard_map/ppermute | solution.py:525
  88.5 0.8 copy-start.2
  105.9 35.7 %collective-permute-start.13 = (bf16[320,768]{1,0:T(8,128)(2,1)}, bf16[320,768]{1,0:T(8,128)(2,1)}, u32[]{:S(2)}, u32[]{:S(2)}) collective-permute-start(bf16[320,768]{1,0:T(8,128)(2,1)} %get-tuple-element.58), channel_id=1, source_target_pairs={{0,6},{1,7},{2,4},{3,5},{4,2},{5,3},{6,0},{7,1},{8,14},{9,15},{10,... | collective-permute-start | bytes 1474568 | tf_op jit(solution)/shard_map/ppermute | solution.py:556
  111.1 31.1 %collective-permute-start.14 = (bf16[320,768]{1,0:T(8,128)(2,1)}, bf16[320,768]{1,0:T(8,128)(2,1)}, u32[]{:S(2)}, u32[]{:S(2)}) collective-permute-start(bf16[320,768]{1,0:T(8,128)(2,1)} %get-tuple-element.59), channel_id=1, source_target_pairs={{0,7},{1,6},{2,5},{3,4},{4,3},{5,2},{6,1},{7,0},{8,15},{9,14},{10,... | collective-permute-start | bytes 1474568 | tf_op jit(solution)/shard_map/ppermute | solution.py:556
  111.1 32.4 %collective-permute-start.10 = (bf16[320,768]{1,0:T(8,128)(2,1)}, bf16[320,768]{1,0:T(8,128)(2,1)}, u32[]{:S(2)}, u32[]{:S(2)}) collective-permute-start(bf16[320,768]{1,0:T(8,128)(2,1)} %get-tuple-element.52), channel_id=1, source_target_pairs={{0,5},{1,4},{2,7},{3,6},{4,1},{5,0},{6,3},{7,2},{8,13},{9,12},{10,... | collective-permute-start | bytes 1474568 | tf_op jit(solution)/shard_map/ppermute | solution.py:553
  129.0 12.6 %collective-permute-start.19 = (bf16[320,768]{1,0:T(8,128)(2,1)}, bf16[320,768]{1,0:T(8,128)(2,1)}, u32[]{:S(2)}, u32[]{:S(2)}) collective-permute-start(bf16[320,768]{1,0:T(8,128)(2,1)} %copy-done.5), channel_id=1, source_target_pairs={{0,8},{8,0},{1,9},{9,1},{2,10},{10,2},{3,11},{11,3},{4,12},{12,4},... | collective-permute-start | bytes 1474568 | tf_op jit(solution)/shard_map/ppermute | solution.py:525
  141.6 29.6 %collective-permute-start.6 = (bf16[320,768]{1,0:T(8,128)(2,1)}, bf16[320,768]{1,0:T(8,128)(2,1)S(1)}, u32[]{:S(2)}, u32[]{:S(2)}) collective-permute-start(bf16[320,768]{1,0:T(8,128)(2,1)} %get-tuple-element.48), channel_id=1, source_target_pairs={{0,1},{1,0},{2,3},{3,2},{4,5},{5,4},{6,7},{7,6},{8,9},{9,8},{10,11... | collective-permute-start | bytes 1474568 | tf_op jit(solution)/shard_map/ppermute | solution.py:553
  141.6 34.6 %collective-permute-start.7 = (bf16[320,768]{1,0:T(8,128)(2,1)}, bf16[320,768]{1,0:T(8,128)(2,1)S(1)}, u32[]{:S(2)}, u32[]{:S(2)}) collective-permute-start(bf16[320,768]{1,0:T(8,128)(2,1)} %get-tuple-element.49), channel_id=1, source_target_pairs={{0,2},{1,3},{2,0},{3,1},{4,6},{5,7},{6,4},{7,5},{8,10},{9,11},{10,... | collective-permute-start | bytes 1474568 | tf_op jit(solution)/shard_map/ppermute | solution.py:553
  142.2 34.1 %collective-permute-start.8 = (bf16[320,768]{1,0:T(8,128)(2,1)}, bf16[320,768]{1,0:T(8,128)(2,1)S(1)}, u32[]{:S(2)}, u32[]{:S(2)}) collective-permute-start(bf16[320,768]{1,0:T(8,128)(2,1)} %get-tuple-element.50), channel_id=1, source_target_pairs={{0,3},{1,2},{2,1},{3,0},{4,7},{5,6},{6,5},{7,4},{8,11},{9,10},{10,... | collective-permute-start | bytes 1474568 | tf_op jit(solution)/shard_map/ppermute | solution.py:553
  143.5 34.8 %collective-permute-start.9 = (bf16[320,768]{1,0:T(8,128)(2,1)}, bf16[320,768]{1,0:T(8,128)(2,1)}, u32[]{:S(2)}, u32[]{:S(2)}) collective-permute-start(bf16[320,768]{1,0:T(8,128)(2,1)} %get-tuple-element.51), channel_id=1, source_target_pairs={{0,4},{1,5},{2,6},{3,7},{4,0},{5,1},{6,2},{7,3},{8,12},{9,13},{10,... | collective-permute-start | bytes 1474568 | tf_op jit(solution)/shard_map/ppermute | solution.py:553
  171.2 7.1 %copy-start.7 = (bf16[320,768]{1,0:T(8,128)(2,1)}, bf16[320,768]{1,0:T(8,128)(2,1)S(1)}, u32[]{:S(2)}) copy-start(bf16[320,768]{1,0:T(8,128)(2,1)S(1)} %collective-permute-done.6.refs_1_) | copy-start | bytes 1474564
  171.2 20.3 %collective-permute-start.20 = (bf16[320,768]{1,0:T(8,128)(2,1)}, bf16[320,768]{1,0:T(8,128)(2,1)S(1)}, u32[]{:S(2)}, u32[]{:S(2)}) collective-permute-start(bf16[320,768]{1,0:T(8,128)(2,1)} %collective-permute-done.2.refs_2_), channel_id=1, source_target_pairs={{0,8},{8,0},{1,9},{9,1},{2,10},{10,2},{3,11},{11,3},{4,12},{12,4},... | collective-permute-start | bytes 1474568 | tf_op jit(solution)/shard_map/ppermute | solution.py:525
  176.2 2.1 copy-start.8
  176.2 22.9 %collective-permute-start.21 = (bf16[320,768]{1,0:T(8,128)(2,1)}, bf16[320,768]{1,0:T(8,128)(2,1)}, u32[]{:S(2)}, u32[]{:S(2)}) collective-permute-start(bf16[320,768]{1,0:T(8,128)(2,1)} %collective-permute-done.3.refs_3_), channel_id=1, source_target_pairs={{0,8},{8,0},{1,9},{9,1},{2,10},{10,2},{3,11},{11,3},{4,12},{12,4},... | collective-permute-start | bytes 1474568 | tf_op jit(solution)/shard_map/ppermute | solution.py:525
  176.3 2.0 copy-start.9
  176.3 33.4 %collective-permute-start.22 = (bf16[320,768]{1,0:T(8,128)(2,1)}, bf16[320,768]{1,0:T(8,128)(2,1)}, u32[]{:S(2)}, u32[]{:S(2)}) collective-permute-start(bf16[320,768]{1,0:T(8,128)(2,1)} %collective-permute-done.4.refs_4_), channel_id=1, source_target_pairs={{0,8},{8,0},{1,9},{9,1},{2,10},{10,2},{3,11},{11,3},{4,12},{12,4},... | collective-permute-start | bytes 1474568 | tf_op jit(solution)/shard_map/ppermute | solution.py:525
  178.2 41.9 %collective-permute-start.23 = (bf16[320,768]{1,0:T(8,128)(2,1)}, bf16[320,768]{1,0:T(8,128)(2,1)}, u32[]{:S(2)}, u32[]{:S(2)}) collective-permute-start(bf16[320,768]{1,0:T(8,128)(2,1)} %collective-permute-done.5.refs_5_), channel_id=1, source_target_pairs={{0,8},{8,0},{1,9},{9,1},{2,10},{10,2},{3,11},{11,3},{4,12},{12,4},... | collective-permute-start | bytes 1474568 | tf_op jit(solution)/shard_map/ppermute | solution.py:525
  178.3 14.0 %copy-start = (bf16[2,320,768]{2,1,0:T(8,128)(2,1)S(1)}, bf16[2,320,768]{2,1,0:T(8,128)(2,1)}, u32[]{:S(2)}) copy-start(bf16[2,320,768]{2,1,0:T(8,128)(2,1)} %pad_maximum_fusion) | copy-start | bytes 2949124
  191.5 0.8 copy-start.6
  192.3 59.9 %collective-permute-start.17 = (bf16[10,64,768]{2,1,0:T(8,128)(2,1)S(1)}, bf16[10,64,768]{2,1,0:T(8,128)(2,1)S(1)}, u32[]{:S(2)}, u32[]{:S(2)}) collective-permute-start(bf16[10,64,768]{2,1,0:T(8,128)(2,1)S(1)} %bitcast.42), channel_id=1, source_target_pairs={{0,8},{8,0},{1,9},{9,1},{2,10},{10,2},{3,11},{11,3},{4,12},{12,4},... | collective-permute-start | bytes 2949128 | tf_op jit(solution)/shard_map/ppermute | solution.py:525
  199.1 53.1 %collective-permute-start.15 = (bf16[320,768]{1,0:T(8,128)(2,1)}, bf16[320,768]{1,0:T(8,128)(2,1)}, u32[]{:S(2)}, u32[]{:S(2)}) collective-permute-start(bf16[320,768]{1,0:T(8,128)(2,1)} %copy-done.2), channel_id=1, source_target_pairs={{0,8},{8,0},{1,9},{9,1},{2,10},{10,2},{3,11},{11,3},{4,12},{12,4},... | collective-permute-start | bytes 1474568 | tf_op jit(solution)/shard_map/ppermute | solution.py:525
  209.7 51.8 %collective-permute-start.16 = (bf16[320,768]{1,0:T(8,128)(2,1)}, bf16[320,768]{1,0:T(8,128)(2,1)}, u32[]{:S(2)}, u32[]{:S(2)}) collective-permute-start(bf16[320,768]{1,0:T(8,128)(2,1)} %collective-permute-done.12.refs_1_.refs_7_), channel_id=1, source_target_pairs={{0,8},{8,0},{1,9},{9,1},{2,10},{10,2},{3,11},{11,3},{4,12},{12,4},... | collective-permute-start | bytes 1474568 | tf_op jit(solution)/shard_map/ppermute | solution.py:525
  252.2 9.3 %copy-start.1 = (bf16[10,64,768]{2,1,0:T(8,128)(2,1)}, bf16[10,64,768]{2,1,0:T(8,128)(2,1)S(1)}, u32[]{:S(2)}) copy-start(bf16[10,64,768]{2,1,0:T(8,128)(2,1)S(1)} %collective-permute-done.17.refs_2_) | copy-start | bytes 2949124
where the time goes:
time: 284 us
  Pallas kernels  164 us (58%)
  waiting for transfers between devices  59 us (21%)
  starting transfers between devices  31.3 us (11%)
  local copies, waits for them, and re-layouts  17.6 us (6%)
  other arithmetic  10.4 us (4%)
    pallas_call x3, Pallas kernels, _dw(): pl.pallas_call(kernel, in_specs=[SMEM] * 3 + [HBM] * (ng + 4 + nadd), out...  80.9 us
    ppermute x11, waiting for transfers between devices, run(): swap = lambda v: lax.ppermute(v, 'data', zswap)  59 us
    pallas_call x2, Pallas kernels, _own_rows(): pl.pallas_call(kernel, in_specs=[SMEM] * 3 + [HBM] * (ng + 5 + (3 if alia...  50.7 us
    ppermute x11, starting transfers between devices, run(): swap = lambda v: lax.ppermute(v, 'data', zswap)  17.2 us
    pallas_call x2, Pallas kernels, _scatter_rows(): pl.pallas_call(kernel, in_specs=[SMEM] + [vm] * 4, out_specs=[HBM] * k, o...  16.8 us
    unnamed x31, local copies, waits for them, and re-layouts  14.1 us
    pallas_call x1, Pallas kernels, _gather_rows(): pl.pallas_call(kernel, grid=(t // tb,), in_specs=[pl.BlockSpec((tb, 1), l...  13.1 us
    ppermute x7, starting transfers between devices, run(): dyd.append(lax.ppermute(send[k], 'expert', xor(k)))  6.3 us
  transfers between devices with their start and end apart: 25, of which 6 were waited for; matrix products, arithmetic and copies ran while one was open for 8% of the time, Pallas kernels for 47%

commit v1 on v0

--- a/solution.py
+++ b/solution.py
@@ -297,35 +297,34 @@
     )(rng, tl, meta, *gs, h1, h3, w1, w3, w2, *(halves if alias else ()))
 
 
-def _plan(occ, occo, meta, cut, tps, size):
+def _plan(occ, meta, cut, tps, size):
     nt = occ.shape[0]
 
-    def kernel(occ_ref, occo_ref, meta_ref, tl_ref, tlo_ref, bnd_ref):
+    def kernel(occ_ref, meta_ref, tl_ref, bnd_ref):
         me = meta_ref[1]
-        for li, (o_ref, t_ref) in enumerate(((occ_ref, tl_ref), (occo_ref, tlo_ref))):
-            pos = jnp.int32(0)
-            bnd_ref[li * 4] = pos
-            for part, (lo, hi) in enumerate(((0, cut * tps), (cut * tps, nt))):
-                def step(t, pos):
-                    t_ref[pos] = t
-                    return pos + o_ref[lax.bitwise_xor(t // tps, me) * tps + lax.rem(t, tps)]
-
-                pos = lax.fori_loop(lo, hi, step, pos)
-                end = ((pos + BT - 1) // BT) * BT
-
-                def pad(i, c):
-                    t_ref[i] = -1
-                    return c
-
-                lax.fori_loop(pos, end if part == 0 else end + BT, pad, 0)
-                pos = end
-                bnd_ref[li * 4 + 1 + part] = pos // BT
-            bnd_ref[li * 4 + 3] = (pos // BT + 1) // 2
+        pos = jnp.int32(0)
+        bnd_ref[0] = pos
+        for part, (lo, hi) in enumerate(((0, cut * tps), (cut * tps, nt))):
+            def step(t, pos):
+                tl_ref[pos] = t
+                return pos + occ_ref[lax.bitwise_xor(t // tps, me) * tps + lax.rem(t, tps)]
+
+            pos = lax.fori_loop(lo, hi, step, pos)
+            end = ((pos + BT - 1) // BT) * BT
+
+            def pad(i, c):
+                tl_ref[i] = -1
+                return c
+
+            lax.fori_loop(pos, end if part == 0 else end + BT, pad, 0)
+            pos = end
+            bnd_ref[1 + part] = pos // BT
+        bnd_ref[3] = (pos // BT + 1) // 2
 
     return pl.pallas_call(
-        kernel, in_specs=[SMEM] * 3, out_specs=[SMEM] * 3,
-        out_shape=[jax.ShapeDtypeStruct((size,), I32), jax.ShapeDtypeStruct((size,), I32), jax.ShapeDtypeStruct((8,), I32)],
-        name="plan", cost_estimate=_cost(1e6, 1e3))(occ, occo, meta)
+        kernel, in_specs=[SMEM] * 2, out_specs=[SMEM] * 2,
+        out_shape=[jax.ShapeDtypeStruct((size,), I32), jax.ShapeDtypeStruct((8,), I32)],
+        name="plan", cost_estimate=_cost(1e6, 1e3))(occ, meta)
 
 
 def _dw(rng, tl, meta, first, gs, x, own, peer, sums, at, bt):
@@ -349,7 +348,7 @@
 
         def xcopy(b, j):
             t = tl_ref[b * bt + j]
-            t = lax.bitwise_xor(t // tps, me) * tps + lax.rem(t, tps) if own else t - first * tps
+            t = lax.bitwise_xor(t // tps, me) * tps + lax.rem(t, tps)
             return pltpu.make_async_copy(x_ref.at[t], xb.at[b - b0, pl.ds(j * tile, tile)], xsem.at[b - b0, j])
 
         gcopies = [pltpu.make_async_copy(g_refs[q], gall.at[pl.ds(q * cap, cap)], gsem.at[q]) for q in range(ng)]
@@ -525,9 +524,7 @@
         swap = lambda v: lax.ppermute(v, 'data', zswap)
 
         x4 = xd.reshape(nt, TILE, d)
-        x8 = xd.reshape(ne, cap, d)
-        xk = [lax.dynamic_index_in_dim(x8, me ^ k, 0, keepdims=True) for k in range(ne)]
-        xo = [swap(jnp.concatenate(xk[i:j], axis=0).reshape((j - i) * tps, TILE, d)) for i, j in ((0, ka), (ka, ne))]
+        xo = swap(x4)
 
         send = [None] * ne
         for ks in groups:
@@ -543,7 +540,8 @@
         occ = jnp.any(x4 != 0, axis=(1, 2)).astype(I32)
         occo = swap(occ)
         nblk = -(-ka * tps // BT) + -(-(ne - ka) * tps // BT) + 1
-        tl, tlo, bnd = _plan(occ, occo, meta, ka, tps, (nblk + 1) * BT)
+        tl, bnd = _plan(occ, meta, ka, tps, (nblk + 1) * BT)
+        tlo, bndo = _plan(occo, meta, ka, tps, (nblk + 1) * BT)
 
         h14, h34 = h1.reshape(nt, TILE, f), h3.reshape(nt, TILE, f)
         wts = (w1[0], w3[0], w2[0])
@@ -558,8 +556,8 @@
         dg = jnp.einsum('tkd,td->tk', yd, dy, preferred_element_type=F32)
         cpos = jnp.where(slot >= 0, (topk_idx ^ me) * cap + slot, -1)
         dx = _gather_rows(cpos, back)
-        sums = _dw(bnd, tlo, meta, 0, dyo[:ka], xo[0], None, wts, sums, (4, 5), BT)
-        sums = _dw(bnd, tlo, meta, ka, dyo[ka:], xo[1], None, wts, sums, (5, 6), BT)
+        sums = _dw(bndo, tlo, meta, 0, dyo[:ka], xo, None, wts, sums, (0, 1), BT)
+        sums = _dw(bndo, tlo, meta, ka, dyo[ka:], xo, None, wts, sums, (1, 2), BT)
         dw1, dw3, dw2 = sums
         return dx, dg, dw1[None], dw3[None], dw2[None]
 

time: 284 us -> 304 us (1.070)
  the two profiles are of different devices: /device:TPU:14 before, /device:TPU:12 now
where the time goes in v1:
time: 304 us
  Pallas kernels  159 us (52%)
  waiting for transfers between devices  77.5 us (25%)
  starting transfers between devices  50.4 us (17%)
  other arithmetic  9.88 us (3%)
  local copies, waits for them, and re-layouts  6.19 us (2%)
    pallas_call x3, Pallas kernels, _dw(): pl.pallas_call(kernel, in_specs=[SMEM] * 3 + [HBM] * (ng + 4 + nadd), out...  81.2 us
    ppermute x10, waiting for transfers between devices, run(): swap = lambda v: lax.ppermute(v, 'data', zswap)  51.4 us
    pallas_call x2, Pallas kernels, _own_rows(): pl.pallas_call(kernel, in_specs=[SMEM] * 3 + [HBM] * (ng + 5 + (3 if alia...  44 us
    ppermute x10, starting transfers between devices, run(): swap = lambda v: lax.ppermute(v, 'data', zswap)  30.7 us
    ppermute x7, waiting for transfers between devices, run(): dyd.append(lax.ppermute(send[k], 'expert', xor(k)))  26.1 us
    pallas_call x2, Pallas kernels, _scatter_rows(): pl.pallas_call(kernel, in_specs=[SMEM] + [vm] * 4, out_specs=[HBM] * k, o...  16.8 us
    pallas_call x1, Pallas kernels, _gather_rows(): pl.pallas_call(kernel, grid=(t // tb,), in_specs=[pl.BlockSpec((tb, 1), l...  13.1 us
    ppermute x2, starting transfers between devices, run(): back.append(lax.ppermute(db[k - ka], 'expert', xor(k)))  9.22 us
  transfers between devices with their start and end apart: 24, of which 6 were waited for; matrix products, arithmetic and copies ran while one was open for 4% of the time, Pallas kernels for 42%

profile of v1, /device:TPU:12, one launch (start us, length us, event | category | flops | bytes accessed | tf_op | source)
XLA Modules:
  0.0 304.0 jit_solution(12825798480577908831)
XLA Ops:
  0.6 2.0 copy.38.g_ref
  2.7 0.7 pad_add_fusion.meta_ref
  3.3 8.4 %scatter_rows.2 = (bf16[320,768]{1,0:T(8,128)(2,1)}, bf16[320,768]{1,0:T(8,128)(2,1)}, bf16[320,768]{1,0:T(8,128)(2,1)}, bf16[320,768]{1,0:T(8,128)(2,1)}) custom-call(s32[2]{0:T(128)} %pad_add_fusion.meta_ref, s32[1,2048]{1,0:T(1,128)} %bitcast.34, s32[1,2048]{1,0:T(1,128)} %bitcast.32, f32[2048,1]{1,0:T(8,128)} %copy.38.g_ref, bf16[2048,768]{1,0:T(8,128)(2,1)} %dy_ref.3), custom_call_target="tpu_custom_call" | custom-call | flops 4026531840 | bytes 3932160 | tf_op jit(solution)/shard_map/scatter_rows/pallas_call | solution.py:76
  11.7 0.0 copy-start.5
  11.7 0.0 copy-start.4
  11.7 0.0 collective-permute-start
  11.8 8.4 %scatter_rows.3 = (bf16[320,768]{1,0:T(8,128)(2,1)}, bf16[320,768]{1,0:T(8,128)(2,1)}, bf16[320,768]{1,0:T(8,128)(2,1)}, bf16[320,768]{1,0:T(8,128)(2,1)}) custom-call(s32[2]{0:T(128)} %pad_add_fusion.meta_ref, s32[1,2048]{1,0:T(1,128)} %bitcast.35, s32[1,2048]{1,0:T(1,128)} %bitcast.33, f32[2048,1]{1,0:T(8,128)} %copy.38.g_ref, bf16[2048,768]{1,0:T(8,128)(2,1)} %dy_ref.3), custom_call_target="tpu_custom_call" | custom-call | flops 4026531840 | bytes 3932160 | tf_op jit(solution)/shard_map/scatter_rows/pallas_call | solution.py:76
  20.2 1.5 collective-permute-start.1
  21.7 0.4 collective-permute-start.2
  22.1 0.5 collective-permute-start.3
  22.6 1.1 collective-permute-start.4
  23.7 0.4 copy.33
  24.1 0.1 xor_multiply_fusion
  24.2 3.0 %compare_reduce_fusion = pred[2560]{0:T(1024)(128)(4,1)S(1)} fusion(bf16[1,2560,768]{2,1,0:T(8,128)(2,1)} %param.16), kind=kLoop, calls=%fused_computation | loop fusion | flops 3929600 | bytes 3934720 | tf_op jit(solution)/shard_map/reduce_or | solution.py:540
  27.3 0.1 reduce_or.14
  27.3 0.1 reduce_or.18
  27.5 0.5 convert_element_type.3.occ_ref
  28.0 0.3 copy.35
  28.3 0.4 copy.37
  28.7 0.5 copy.36
  29.2 1.9 plan.2
  31.1 4.3 %fusion = f32[2048]{0:T(1024)} fusion(bf16[2048,768]{1,0:T(8,128)(2,1)} %dy_ref.3, bf16[2048,1,768]{2,0,1:T(8,128)(2,1)} %param.15), kind=kLoop, calls=%fused_computation.2 | loop fusion | flops 6289408 | bytes 6299648 | tf_op jit(solution)/shard_map/tkd,td->tk/dot_general | solution.py:556
  35.5 0.0 collective-permute-done.refs_1_
  35.5 0.5 collective-permute-start.14
  35.9 0.8 copy-done.6
  36.7 1.4 collective-permute-start.10
  38.1 6.1 %collective-permute-done.2.refs_3_ = bf16[320,768]{1,0:T(8,128)(2,1)} collective-permute-done((bf16[320,768]{1,0:T(8,128)(2,1)}, bf16[320,768]{1,0:T(8,128)(2,1)}, u32[]{:S(2)}, u32[]{:S(2)}) %collective-permute-start.2) | collective-permute-done | bytes 491552 | tf_op jit(solution)/shard_map/ppermute | solution.py:535
  44.2 2.1 collective-permute-start.11
  46.3 0.4 collective-permute-start.18
  46.8 20.0 %collective-permute-done.4.refs_5_ = bf16[320,768]{1,0:T(8,128)(2,1)} collective-permute-done((bf16[320,768]{1,0:T(8,128)(2,1)}, bf16[320,768]{1,0:T(8,128)(2,1)}, u32[]{:S(2)}, u32[]{:S(2)}) %collective-permute-start.4) | collective-permute-done | bytes 491552 | tf_op jit(solution)/shard_map/ppermute | solution.py:535
  66.7 0.4 collective-permute-start.17
  67.2 34.1 %own_rows.2 = (bf16[320,768]{1,0:T(8,128)(2,1)}, bf16[320,768]{1,0:T(8,128)(2,1)}, bf16[320,768]{1,0:T(8,128)(2,1)}, bf16[320,768]{1,0:T(8,128)(2,1)}, bf16[320,...) custom-call(s32[8]{0:T(128)} %get-tuple-element.40.rng_ref, ...), custom_call_target="tpu_custom_call" | custom-call | flops 16986931200 | bytes 50000000 | tf_op jit(solution)/shard_map/own_rows/pallas_call | solution.py:284
  101.3 0.0 collective-permute-done.10.refs_0_.refs_6_
  101.3 0.0 collective-permute-done.11.refs_1_.refs_7_
  101.4 0.8 copy-done.2
  102.1 9.9 %own_rows.3 = (bf16[320,768]{1,0:T(8,128)(2,1)}, bf16[320,768]{1,0:T(8,128)(2,1)}, bf16[3072,1536]{1,0:T(8,128)(2,1)}, bf16[3072,1536]{1,0:T(8,128)(2,1)}, bf16[3072,1536]{1,0:T(8,128)(2,1)}) custom-call(s32[8]{0:T(128)} %get-tuple-element.40.rng_ref, s32[52]{0:T(128)} %get-tuple-element.41.tl_ref, ...), custom_call_target="tpu_custom_call", output_to_operand_aliasing={{2}: (10, {}), {3}: (11, {}), {4}: (12, {})} | custom-call | flops 5662310400 | bytes 50000000 | tf_op jit(solution)/shard_map/own_rows/pallas_call | solution.py:284
  112.0 0.0 collective-permute-start.12
  112.0 9.2 %collective-permute-start.13 = (bf16[320,768]{1,0:T(8,128)(2,1)}, bf16[320,768]{1,0:T(8,128)(2,1)S(1)}, u32[]{:S(2)}, u32[]{:S(2)}) collective-permute-start(bf16[320,768]{1,0:T(8,128)(2,1)} %get-tuple-element.60), channel_id=1, source_target_pairs={{0,7},{1,6},{2,5},{3,4},{4,3},{5,2},{6,1},{7,0},{8,15},{9,14},{10,... | collective-permute-start | bytes 1474568 | tf_op jit(solution)/shard_map/ppermute | solution.py:554
  121.2 0.0 collective-permute-done.14.occ_ref
  121.2 0.0 collective-permute-start.5
  121.2 13.7 %collective-permute-start.19 = (bf16[320,768]{1,0:T(8,128)(2,1)}, bf16[320,768]{1,0:T(8,128)(2,1)S(1)}, u32[]{:S(2)}, u32[]{:S(2)}) collective-permute-start(bf16[320,768]{1,0:T(8,128)(2,1)} %collective-permute-done.refs_1_), channel_id=1, source_target_pairs={{0,8},{8,0},{1,9},{9,1},{2,10},{10,2},{3,11},{11,3},{4,12},{12,4},... | collective-permute-start | bytes 1474568 | tf_op jit(solution)/shard_map/ppermute | solution.py:524
  134.9 1.1 broadcast_select_fusion.pos_ref
  136.1 1.9 plan.3
  138.0 26.9 %collective-permute-done.19.refs_1_ = bf16[320,768]{1,0:T(8,128)(2,1)S(1)} collective-permute-done((bf16[320,768]{1,0:T(8,128)(2,1)}, bf16[320,768]{1,0:T(8,128)(2,1)S(1)}, u32[]{:S(2)}, u32[]{:S(2)}) %collective-permute-start.19) | collective-permute-done | bytes 491552 | tf_op jit(solution)/shard_map/ppermute | solution.py:524
  164.8 1.5 collective-permute-start.6
  166.3 0.0 collective-permute-done.12.refs_6_
  166.3 0.0 collective-permute-start.7
  166.4 0.5 collective-permute-start.8
  166.9 1.4 collective-permute-start.9
  168.4 22.6 %own_dw.1 = (f32[768,1536]{1,0:T(8,128)}, f32[768,1536]{1,0:T(8,128)}, f32[1536,768]{1,0:T(8,128)}) custom-call(s32[8]{0:T(128)} %get-tuple-element.40.rng_ref, s32[52]{0:T(128)} %get-tuple-element.41.tl_ref, s32[2]{0:T(128)} %pad_add_fusion.meta_ref, bf16[320,768]{1,0:T(8,128)(2,1)} %get-tuple-element.42.refs_0_, ...), custom_call_target="tpu_custom_call" | custom-call | flops 11324620800 | bytes 50000000 | tf_op jit(solution)/shard_map/own_dw/pallas_call | solution.py:492
  191.0 9.5 %collective-permute-start.20 = (bf16[320,768]{1,0:T(8,128)(2,1)S(1)}, bf16[320,768]{1,0:T(8,128)(2,1)S(1)}, u32[]{:S(2)}, u32[]{:S(2)}) collective-permute-start(bf16[320,768]{1,0:T(8,128)(2,1)S(1)} %copy-done.7), channel_id=1, source_target_pairs={{0,8},{8,0},{1,9},{9,1},{2,10},{10,2},{3,11},{11,3},{4,12},{12,4},... | collective-permute-start | bytes 1474568 | tf_op jit(solution)/shard_map/ppermute | solution.py:524
  200.5 0.1 collective-permute-start.21
  200.5 2.0 collective-permute-start.22
  202.5 0.1 collective-permute-start.23
  202.6 13.1 %gather_rows.1 = bf16[2048,768]{1,0:T(8,128)(2,1)} custom-call(s32[2048,1]{1,0:T(8,128)} %broadcast_select_fusion.pos_ref, bf16[320,768]{1,0:T(8,128)(2,1)} %get-tuple-element.48.refs_0_, bf16[320,768]{1,0:T(8,128)(2,1)} %copy-done.11, bf16[320,768]{1,0:T(8,128)(2,1)} %copy-done.12, bf16[320,768]{1,0:T(8,128)(2,1)} %copy-done.14, ...), custom_call_target="tpu_custom_call" | custom-call | flops 8053063680 | bytes 7864320 | tf_op jit(solution)/shard_map/gather_rows/pallas_call | solution.py:105
  215.7 2.0 collective-permute-start.15
  217.7 5.5 %collective-permute-done.21.refs_3_ = bf16[320,768]{1,0:T(8,128)(2,1)} collective-permute-done((bf16[320,768]{1,0:T(8,128)(2,1)}, bf16[320,768]{1,0:T(8,128)(2,1)}, u32[]{:S(2)}, u32[]{:S(2)}) %collective-permute-start.21) | collective-permute-done | bytes 491552 | tf_op jit(solution)/shard_map/ppermute | solution.py:524
  223.2 2.0 collective-permute-start.16
  225.2 8.5 %collective-permute-done.22.refs_4_ = bf16[320,768]{1,0:T(8,128)(2,1)} collective-permute-done((bf16[320,768]{1,0:T(8,128)(2,1)}, bf16[320,768]{1,0:T(8,128)(2,1)}, u32[]{:S(2)}, u32[]{:S(2)}) %collective-permute-start.22) | collective-permute-done | bytes 491552 | tf_op jit(solution)/shard_map/ppermute | solution.py:524
  233.7 10.5 %collective-permute-done.23.refs_5_ = bf16[320,768]{1,0:T(8,128)(2,1)} collective-permute-done((bf16[320,768]{1,0:T(8,128)(2,1)}, bf16[320,768]{1,0:T(8,128)(2,1)}, u32[]{:S(2)}, u32[]{:S(2)}) %collective-permute-start.23) | collective-permute-done | bytes 491552 | tf_op jit(solution)/shard_map/ppermute | solution.py:524
  244.2 36.6 %peer_dw.2 = (f32[768,1536]{1,0:T(8,128)}, f32[768,1536]{1,0:T(8,128)}, f32[1536,768]{1,0:T(8,128)}) custom-call(s32[8]{0:T(128)} %get-tuple-element.61.rng_ref, s32[52]{0:T(128)} %get-tuple-element.62.tl_ref, s32[2]{0:T(128)} %pad_add_fusion.meta_ref, bf16[320,768]{1,0:T(8,128)(2,1)} %collective-permute-done.18.refs_0_, bf16[320,768]{1,0:T(8,128)(2,1)} %copy-done.8, ...), custom_call_target="tpu_custom_call" | custom-call | flops 16986931200 | bytes 50000000 | tf_op jit(solution)/shard_map/peer_dw/pallas_call | solution.py:492
  280.9 0.8 copy-done
  281.7 0.2 copy-done.1
  281.8 22.0 %peer_dw.3 = (f32[768,1536]{1,0:T(8,128)}, f32[768,1536]{1,0:T(8,128)}, f32[1536,768]{1,0:T(8,128)}) custom-call(s32[8]{0:T(128)} %get-tuple-element.61.rng_ref, s32[52]{0:T(128)} %get-tuple-element.62.tl_ref, s32[2]{0:T(128)} %pad_add_fusion.meta_ref, bf16[320,768]{1,0:T(8,128)(2,1)} %copy-done, bf16[320,768]{1,0:T(8,128)(2,1)} %copy-done.1, ...), custom_call_target="tpu_custom_call" | custom-call | flops 5662310400 | bytes 50000000 | tf_op jit(solution)/shard_map/peer_dw/pallas_call | solution.py:492
  (43 shorter events, 0.1 us)
Async XLA Ops:
  11.7 12.0 %copy-start.5 = (s32[2048,1]{0,1:T(1,128)S(1)}, s32[2048,1]{0,1:T(1,128)}, u32[]{:S(2)}) copy-start(s32[2048,1]{0,1:T(1,128)} %param.13) | copy-start | bytes 24580
  11.7 12.4 %copy-start.4 = (s32[2048,1]{0,1:T(1,128)S(1)}, s32[2048,1]{0,1:T(1,128)}, u32[]{:S(2)}) copy-start(s32[2048,1]{0,1:T(1,128)} %param.14) | copy-start | bytes 24580
  11.7 23.7 %collective-permute-start = (bf16[320,768]{1,0:T(8,128)(2,1)}, bf16[320,768]{1,0:T(8,128)(2,1)}, u32[]{:S(2)}, u32[]{:S(2)}) collective-permute-start(bf16[320,768]{1,0:T(8,128)(2,1)} %get-tuple-element.43), channel_id=1, source_target_pairs={{0,1},{1,0},{2,3},{3,2},{4,5},{5,4},{6,7},{7,6},{8,9},{9,8},{10,11... | collective-permute-start | bytes 1474568 | tf_op jit(solution)/shard_map/ppermute | solution.py:535
  20.2 15.7 %collective-permute-start.1 = (bf16[320,768]{1,0:T(8,128)(2,1)}, bf16[320,768]{1,0:T(8,128)(2,1)S(1)}, u32[]{:S(2)}, u32[]{:S(2)}) collective-permute-start(bf16[320,768]{1,0:T(8,128)(2,1)} %get-tuple-element.44), channel_id=1, source_target_pairs={{0,2},{1,3},{2,0},{3,1},{4,6},{5,7},{6,4},{7,5},{8,10},{9,11},{10,... | collective-permute-start | bytes 1474568 | tf_op jit(solution)/shard_map/ppermute | solution.py:535
  21.7 22.5 %collective-permute-start.2 = (bf16[320,768]{1,0:T(8,128)(2,1)}, bf16[320,768]{1,0:T(8,128)(2,1)}, u32[]{:S(2)}, u32[]{:S(2)}) collective-permute-start(bf16[320,768]{1,0:T(8,128)(2,1)} %get-tuple-element.45), channel_id=1, source_target_pairs={{0,3},{1,2},{2,1},{3,0},{4,7},{5,6},{6,5},{7,4},{8,11},{9,10},{10,... | collective-permute-start | bytes 1474568 | tf_op jit(solution)/shard_map/ppermute | solution.py:535
  22.1 24.3 %collective-permute-start.3 = (bf16[320,768]{1,0:T(8,128)(2,1)}, bf16[320,768]{1,0:T(8,128)(2,1)}, u32[]{:S(2)}, u32[]{:S(2)}) collective-permute-start(bf16[320,768]{1,0:T(8,128)(2,1)} %get-tuple-element.46), channel_id=1, source_target_pairs={{0,4},{1,5},{2,6},{3,7},{4,0},{5,1},{6,2},{7,3},{8,12},{9,13},{10,... | collective-permute-start | bytes 1474568 | tf_op jit(solution)/shard_map/ppermute | solution.py:535
  22.6 44.2 %collective-permute-start.4 = (bf16[320,768]{1,0:T(8,128)(2,1)}, bf16[320,768]{1,0:T(8,128)(2,1)}, u32[]{:S(2)}, u32[]{:S(2)}) collective-permute-start(bf16[320,768]{1,0:T(8,128)(2,1)} %get-tuple-element.47), channel_id=1, source_target_pairs={{0,5},{1,4},{2,7},{3,6},{4,1},{5,0},{6,3},{7,2},{8,13},{9,12},{10,... | collective-permute-start | bytes 1474568 | tf_op jit(solution)/shard_map/ppermute | solution.py:535
  28.0 7.5 %copy-start.15 = (s32[40]{0:T(128)S(1)}, s32[40]{0:T(128)}, u32[]{:S(2)}) copy-start(s32[40]{0:T(128)} %convert_element_type.3.occ_ref) | copy-start | bytes 484
  35.5 85.8 %collective-permute-start.14 = (s32[40]{0:T(128)S(1)}, s32[40]{0:T(128)S(1)}, u32[]{:S(2)}, u32[]{:S(2)}) collective-permute-start(s32[40]{0:T(128)S(1)} %copy-done.15), channel_id=1, source_target_pairs={{0,8},{8,0},{1,9},{9,1},{2,10},{10,2},{3,11},{11,3},{4,12},{12,4},... | collective-permute-start | bytes 488 | tf_op jit(solution)/shard_map/ppermute | solution.py:524
  35.9 0.8 copy-start.6
  36.7 64.6 %collective-permute-start.10 = (bf16[320,768]{1,0:T(8,128)(2,1)}, bf16[320,768]{1,0:T(8,128)(2,1)S(1)}, u32[]{:S(2)}, u32[]{:S(2)}) collective-permute-start(bf16[320,768]{1,0:T(8,128)(2,1)} %get-tuple-element.54), channel_id=1, source_target_pairs={{0,6},{1,7},{2,4},{3,5},{4,2},{5,3},{6,0},{7,1},{8,14},{9,15},{10,... | collective-permute-start | bytes 1474568 | tf_op jit(solution)/shard_map/ppermute | solution.py:535
  44.2 57.1 %collective-permute-start.11 = (bf16[320,768]{1,0:T(8,128)(2,1)}, bf16[320,768]{1,0:T(8,128)(2,1)}, u32[]{:S(2)}, u32[]{:S(2)}) collective-permute-start(bf16[320,768]{1,0:T(8,128)(2,1)} %get-tuple-element.55), channel_id=1, source_target_pairs={{0,7},{1,6},{2,5},{3,4},{4,3},{5,2},{6,1},{7,0},{8,15},{9,14},{10,... | collective-permute-start | bytes 1474568 | tf_op jit(solution)/shard_map/ppermute | solution.py:535
  46.3 74.9 %collective-permute-start.18 = (bf16[320,768]{1,0:T(8,128)(2,1)}, bf16[320,768]{1,0:T(8,128)(2,1)}, u32[]{:S(2)}, u32[]{:S(2)}) collective-permute-start(bf16[320,768]{1,0:T(8,128)(2,1)} %get-tuple-element.42.refs_0_), channel_id=1, source_target_pairs={{0,8},{8,0},{1,9},{9,1},{2,10},{10,2},{3,11},{11,3},{4,12},{12,4},... | collective-permute-start | bytes 1474568 | tf_op jit(solution)/shard_map/ppermute | solution.py:524
  66.7 177.5 %collective-permute-start.17 = (bf16[40,64,768]{2,1,0:T(8,128)(2,1)}, bf16[40,64,768]{2,1,0:T(8,128)(2,1)}, u32[]{:S(2)}, u32[]{:S(2)}) collective-permute-start(bf16[40,64,768]{2,1,0:T(8,128)(2,1)} %bitcast.11.refs_8_), channel_id=1, source_target_pairs={{0,8},{8,0},{1,9},{9,1},{2,10},{10,2},{3,11},{11,3},{4,12},{12,4},... | collective-permute-start | bytes 11796488 | tf_op jit(solution)/shard_map/ppermute | solution.py:524
  101.3 0.8 copy-start.2
  112.0 54.3 %collective-permute-start.12 = (bf16[320,768]{1,0:T(8,128)(2,1)}, bf16[320,768]{1,0:T(8,128)(2,1)S(1)}, u32[]{:S(2)}, u32[]{:S(2)}) collective-permute-start(bf16[320,768]{1,0:T(8,128)(2,1)} %get-tuple-element.59), channel_id=1, source_target_pairs={{0,6},{1,7},{2,4},{3,5},{4,2},{5,3},{6,0},{7,1},{8,14},{9,15},{10,... | collective-permute-start | bytes 1474568 | tf_op jit(solution)/shard_map/ppermute | solution.py:554
  112.0 54.3 %collective-permute-start.13 = (bf16[320,768]{1,0:T(8,128)(2,1)}, bf16[320,768]{1,0:T(8,128)(2,1)S(1)}, u32[]{:S(2)}, u32[]{:S(2)}) collective-permute-start(bf16[320,768]{1,0:T(8,128)(2,1)} %get-tuple-element.60), channel_id=1, source_target_pairs={{0,7},{1,6},{2,5},{3,4},{4,3},{5,2},{6,1},{7,0},{8,15},{9,14},{10,... | collective-permute-start | bytes 1474568 | tf_op jit(solution)/shard_map/ppermute | solution.py:554
  121.2 14.8 %copy-start.16 = (s32[40]{0:T(128)}, s32[40]{0:T(128)S(1)}, u32[]{:S(2)}) copy-start(s32[40]{0:T(128)S(1)} %collective-permute-done.14.occ_ref) | copy-start | bytes 484
  121.2 45.7 %collective-permute-start.5 = (bf16[320,768]{1,0:T(8,128)(2,1)}, bf16[320,768]{1,0:T(8,128)(2,1)S(1)}, u32[]{:S(2)}, u32[]{:S(2)}) collective-permute-start(bf16[320,768]{1,0:T(8,128)(2,1)} %get-tuple-element.49), channel_id=1, source_target_pairs={{0,1},{1,0},{2,3},{3,2},{4,5},{5,4},{6,7},{7,6},{8,9},{9,8},{10,11... | collective-permute-start | bytes 1474568 | tf_op jit(solution)/shard_map/ppermute | solution.py:551
  121.2 43.6 %collective-permute-start.19 = (bf16[320,768]{1,0:T(8,128)(2,1)}, bf16[320,768]{1,0:T(8,128)(2,1)S(1)}, u32[]{:S(2)}, u32[]{:S(2)}) collective-permute-start(bf16[320,768]{1,0:T(8,128)(2,1)} %collective-permute-done.refs_1_), channel_id=1, source_target_pairs={{0,8},{8,0},{1,9},{9,1},{2,10},{10,2},{3,11},{11,3},{4,12},{12,4},... | collective-permute-start | bytes 1474568 | tf_op jit(solution)/shard_map/ppermute | solution.py:524
  164.8 26.1 %copy-start.8 = (bf16[320,768]{1,0:T(8,128)(2,1)}, bf16[320,768]{1,0:T(8,128)(2,1)S(1)}, u32[]{:S(2)}) copy-start(bf16[320,768]{1,0:T(8,128)(2,1)S(1)} %collective-permute-done.19.refs_1_) | copy-start | bytes 1474564
  164.8 26.1 %collective-permute-start.6 = (bf16[320,768]{1,0:T(8,128)(2,1)}, bf16[320,768]{1,0:T(8,128)(2,1)S(1)}, u32[]{:S(2)}, u32[]{:S(2)}) collective-permute-start(bf16[320,768]{1,0:T(8,128)(2,1)} %get-tuple-element.50), channel_id=1, source_target_pairs={{0,2},{1,3},{2,0},{3,1},{4,6},{5,7},{6,4},{7,5},{8,10},{9,11},{10,... | collective-permute-start | bytes 1474568 | tf_op jit(solution)/shard_map/ppermute | solution.py:551
  166.3 2.0 copy-start.9
  166.3 34.1 %collective-permute-start.7 = (bf16[320,768]{1,0:T(8,128)(2,1)}, bf16[320,768]{1,0:T(8,128)(2,1)S(1)}, u32[]{:S(2)}, u32[]{:S(2)}) collective-permute-start(bf16[320,768]{1,0:T(8,128)(2,1)} %get-tuple-element.51), channel_id=1, source_target_pairs={{0,3},{1,2},{2,1},{3,0},{4,7},{5,6},{6,5},{7,4},{8,11},{9,10},{10,... | collective-permute-start | bytes 1474568 | tf_op jit(solution)/shard_map/ppermute | solution.py:551
  166.4 2.0 copy-start.10
  166.4 34.2 %collective-permute-start.8 = (bf16[320,768]{1,0:T(8,128)(2,1)}, bf16[320,768]{1,0:T(8,128)(2,1)}, u32[]{:S(2)}, u32[]{:S(2)}) collective-permute-start(bf16[320,768]{1,0:T(8,128)(2,1)} %get-tuple-element.52), channel_id=1, source_target_pairs={{0,4},{1,5},{2,6},{3,7},{4,0},{5,1},{6,2},{7,3},{8,12},{9,13},{10,... | collective-permute-start | bytes 1474568 | tf_op jit(solution)/shard_map/ppermute | solution.py:551
  166.9 1.4 copy-start.11
  166.9 35.6 %collective-permute-start.9 = (bf16[320,768]{1,0:T(8,128)(2,1)}, bf16[320,768]{1,0:T(8,128)(2,1)}, u32[]{:S(2)}, u32[]{:S(2)}) collective-permute-start(bf16[320,768]{1,0:T(8,128)(2,1)} %get-tuple-element.53), channel_id=1, source_target_pairs={{0,5},{1,4},{2,7},{3,6},{4,1},{5,0},{6,3},{7,2},{8,13},{9,12},{10,... | collective-permute-start | bytes 1474568 | tf_op jit(solution)/shard_map/ppermute | solution.py:551
  168.4 22.6 %copy-start.7 = (bf16[320,768]{1,0:T(8,128)(2,1)S(1)}, bf16[320,768]{1,0:T(8,128)(2,1)}, u32[]{:S(2)}) copy-start(bf16[320,768]{1,0:T(8,128)(2,1)} %copy-done.6) | copy-start | bytes 1474564
  191.0 11.6 %copy-start.12 = (bf16[320,768]{1,0:T(8,128)(2,1)}, bf16[320,768]{1,0:T(8,128)(2,1)S(1)}, u32[]{:S(2)}) copy-start(bf16[320,768]{1,0:T(8,128)(2,1)S(1)} %collective-permute-done.6.refs_2_) | copy-start | bytes 1474564
  191.0 24.7 %collective-permute-start.20 = (bf16[320,768]{1,0:T(8,128)(2,1)S(1)}, bf16[320,768]{1,0:T(8,128)(2,1)S(1)}, u32[]{:S(2)}, u32[]{:S(2)}) collective-permute-start(bf16[320,768]{1,0:T(8,128)(2,1)S(1)} %copy-done.7), channel_id=1, source_target_pairs={{0,8},{8,0},{1,9},{9,1},{2,10},{10,2},{3,11},{11,3},{4,12},{12,4},... | collective-permute-start | bytes 1474568 | tf_op jit(solution)/shard_map/ppermute | solution.py:524
  200.5 2.1 copy-start.14
  200.5 22.7 %collective-permute-start.21 = (bf16[320,768]{1,0:T(8,128)(2,1)}, bf16[320,768]{1,0:T(8,128)(2,1)}, u32[]{:S(2)}, u32[]{:S(2)}) collective-permute-start(bf16[320,768]{1,0:T(8,128)(2,1)} %collective-permute-done.2.refs_3_), channel_id=1, source_target_pairs={{0,8},{8,0},{1,9},{9,1},{2,10},{10,2},{3,11},{11,3},{4,12},{12,4},... | collective-permute-start | bytes 1474568 | tf_op jit(solution)/shard_map/ppermute | solution.py:524
  200.5 33.2 %collective-permute-start.22 = (bf16[320,768]{1,0:T(8,128)(2,1)}, bf16[320,768]{1,0:T(8,128)(2,1)}, u32[]{:S(2)}, u32[]{:S(2)}) collective-permute-start(bf16[320,768]{1,0:T(8,128)(2,1)} %collective-permute-done.3.refs_4_), channel_id=1, source_target_pairs={{0,8},{8,0},{1,9},{9,1},{2,10},{10,2},{3,11},{11,3},{4,12},{12,4},... | collective-permute-start | bytes 1474568 | tf_op jit(solution)/shard_map/ppermute | solution.py:524
  202.5 41.7 %collective-permute-start.23 = (bf16[320,768]{1,0:T(8,128)(2,1)}, bf16[320,768]{1,0:T(8,128)(2,1)}, u32[]{:S(2)}, u32[]{:S(2)}) collective-permute-start(bf16[320,768]{1,0:T(8,128)(2,1)} %collective-permute-done.4.refs_5_), channel_id=1, source_target_pairs={{0,8},{8,0},{1,9},{9,1},{2,10},{10,2},{3,11},{11,3},{4,12},{12,4},... | collective-permute-start | bytes 1474568 | tf_op jit(solution)/shard_map/ppermute | solution.py:524
  202.6 13.1 %copy-start.3 = (bf16[320,768]{1,0:T(8,128)(2,1)S(1)}, bf16[320,768]{1,0:T(8,128)(2,1)}, u32[]{:S(2)}) copy-start(bf16[320,768]{1,0:T(8,128)(2,1)} %copy-done.2) | copy-start | bytes 1474564
  215.7 28.5 %copy-start.13 = (bf16[320,768]{1,0:T(8,128)(2,1)}, bf16[320,768]{1,0:T(8,128)(2,1)S(1)}, u32[]{:S(2)}) copy-start(bf16[320,768]{1,0:T(8,128)(2,1)S(1)} %collective-permute-done.20.refs_2_) | copy-start | bytes 1474564
  215.7 65.2 %collective-permute-start.15 = (bf16[320,768]{1,0:T(8,128)(2,1)S(1)}, bf16[320,768]{1,0:T(8,128)(2,1)S(1)}, u32[]{:S(2)}, u32[]{:S(2)}) collective-permute-start(bf16[320,768]{1,0:T(8,128)(2,1)S(1)} %copy-done.3), channel_id=1, source_target_pairs={{0,8},{8,0},{1,9},{9,1},{2,10},{10,2},{3,11},{11,3},{4,12},{12,4},... | collective-permute-start | bytes 1474568 | tf_op jit(solution)/shard_map/ppermute | solution.py:524
  223.2 57.7 %collective-permute-start.16 = (bf16[320,768]{1,0:T(8,128)(2,1)}, bf16[320,768]{1,0:T(8,128)(2,1)S(1)}, u32[]{:S(2)}, u32[]{:S(2)}) collective-permute-start(bf16[320,768]{1,0:T(8,128)(2,1)} %collective-permute-done.11.refs_1_.refs_7_), channel_id=1, source_target_pairs={{0,8},{8,0},{1,9},{9,1},{2,10},{10,2},{3,11},{11,3},{4,12},{12,4},... | collective-permute-start | bytes 1474568 | tf_op jit(solution)/shard_map/ppermute | solution.py:524
  280.9 0.8 copy-start
  280.9 0.9 copy-start.1

commit v2 on v1

--- a/solution.py
+++ b/solution.py
@@ -55,7 +55,9 @@
 
     def kernel(meta_ref, e_ref, s_ref, g_ref, dy_ref, *refs):
         outs, v_ref, ob, sem = refs[:k], refs[k], refs[k + 1], refs[k + 2]
-        v_ref[...] = (g_ref[...] * dy_ref[...].astype(F32)).astype(BF16)
+        col = jnp.broadcast_to(g_ref[...], (128, t)).T
+        for c in range(0, d, 128):
+            v_ref[:, c:c + 128] = (col * dy_ref[:, c:c + 128].astype(F32)).astype(BF16)
 
         @pl.loop(0, k)
         def _(q):
@@ -528,7 +530,7 @@
 
         send = [None] * ne
         for ks in groups:
-            for k, v in zip(ks, _scatter_rows(topk_idx.reshape(1, t), slot.reshape(1, t), gates, dy, meta, ks, cap)):
+            for k, v in zip(ks, _scatter_rows(topk_idx.reshape(1, t), slot.reshape(1, t), gates.reshape(1, t), dy, meta, ks, cap)):
                 send[k] = v
         dyd = [send[0]]
         for k in range(1, ne):

time: 304 us -> 302 us (level)
  transfers between devices with their start and end apart: 24 -> 24, of which waited for: 6 -> 6; matrix products, arithmetic and copies ran while one was open for 4% -> 4% of each run, Pallas kernels for 42% -> 43%
where the time goes in v2:
time: 302 us
  Pallas kernels  159 us (53%)
  waiting for transfers between devices  77.4 us (26%)
  starting transfers between devices  50.3 us (17%)
  other arithmetic  9.84 us (3%)
  local copies, waits for them, and re-layouts  4.18 us (1%)
    pallas_call x3, Pallas kernels, _dw(): pl.pallas_call(kernel, in_specs=[SMEM] * 3 + [HBM] * (ng + 4 + nadd), out...  81.2 us
    ppermute x10, waiting for transfers between devices, run(): swap = lambda v: lax.ppermute(v, 'data', zswap)  51.4 us
    pallas_call x2, Pallas kernels, _own_rows(): pl.pallas_call(kernel, in_specs=[SMEM] * 3 + [HBM] * (ng + 5 + (3 if alia...  44.1 us
    ppermute x10, starting transfers between devices, run(): swap = lambda v: lax.ppermute(v, 'data', zswap)  30.5 us
    ppermute x7, waiting for transfers between devices, run(): dyd.append(lax.ppermute(send[k], 'expert', xor(k)))  26 us
    pallas_call x2, Pallas kernels, _scatter_rows(): pl.pallas_call(kernel, in_specs=[SMEM] + [vm] * 4, out_specs=[HBM] * k, o...  16.4 us
    pallas_call x1, Pallas kernels, _gather_rows(): pl.pallas_call(kernel, grid=(t // tb,), in_specs=[pl.BlockSpec((tb, 1), l...  13.1 us
    ppermute x2, starting transfers between devices, run(): back.append(lax.ppermute(db[k - ka], 'expert', xor(k)))  9.22 us
  transfers between devices with their start and end apart: 24, of which 6 were waited for; matrix products, arithmetic and copies ran while one was open for 4% of the time, Pallas kernels for 43%

profile of v2, /device:TPU:12, one launch (start us, length us, event | category | flops | bytes accessed | tf_op | source)
XLA Modules:
  0.0 301.5 jit_solution(158628704788194396)
XLA Ops:
  0.6 0.6 pad_add_fusion.meta_ref
  1.2 8.2 %scatter_rows.2 = (bf16[320,768]{1,0:T(8,128)(2,1)}, bf16[320,768]{1,0:T(8,128)(2,1)}, bf16[320,768]{1,0:T(8,128)(2,1)}, bf16[320,768]{1,0:T(8,128)(2,1)}) custom-call(s32[2]{0:T(128)} %pad_add_fusion.meta_ref, s32[1,2048]{1,0:T(1,128)} %bitcast.35, s32[1,2048]{1,0:T(1,128)} %bitcast.33, f32[1,2048]{1,0:T(1,128)} %bitcast.41, bf16[2048,768]{1,0:T(8,128)(2,1)} %dy_ref.3), custom_call_target="tpu_custom_call" | custom-call | flops 4026531840 | bytes 3932160 | tf_op jit(solution)/shard_map/scatter_rows/pallas_call | solution.py:78
  9.4 0.0 copy-start.5
  9.4 0.0 copy-start.4
  9.4 0.0 collective-permute-start
  9.5 8.2 %scatter_rows.3 = (bf16[320,768]{1,0:T(8,128)(2,1)}, bf16[320,768]{1,0:T(8,128)(2,1)}, bf16[320,768]{1,0:T(8,128)(2,1)}, bf16[320,768]{1,0:T(8,128)(2,1)}) custom-call(s32[2]{0:T(128)} %pad_add_fusion.meta_ref, s32[1,2048]{1,0:T(1,128)} %bitcast.36, s32[1,2048]{1,0:T(1,128)} %bitcast.34, f32[1,2048]{1,0:T(1,128)} %bitcast.42, bf16[2048,768]{1,0:T(8,128)(2,1)} %dy_ref.3), custom_call_target="tpu_custom_call" | custom-call | flops 4026531840 | bytes 3932160 | tf_op jit(solution)/shard_map/scatter_rows/pallas_call | solution.py:78
  17.7 1.5 collective-permute-start.1
  19.2 0.4 collective-permute-start.2
  19.6 0.5 collective-permute-start.3
  20.1 1.1 collective-permute-start.4
  21.2 0.4 copy.29
  21.6 0.1 xor_multiply_fusion
  21.7 3.0 %compare_reduce_fusion = pred[2560]{0:T(1024)(128)(4,1)S(1)} fusion(bf16[1,2560,768]{2,1,0:T(8,128)(2,1)} %param.16), kind=kLoop, calls=%fused_computation | loop fusion | flops 3929600 | bytes 3934720 | tf_op jit(solution)/shard_map/reduce_or | solution.py:542
  24.8 0.1 reduce_or.14
  24.8 0.1 reduce_or.18
  25.0 0.5 convert_element_type.3.occ_ref
  25.5 0.3 copy.31
  25.9 0.4 copy.33
  26.2 0.5 copy.32
  26.7 1.9 plan.2
  28.6 4.3 %fusion = f32[2048]{0:T(1024)} fusion(bf16[2048,768]{1,0:T(8,128)(2,1)} %dy_ref.3, bf16[2048,1,768]{2,0,1:T(8,128)(2,1)} %param.15), kind=kLoop, calls=%fused_computation.2 | loop fusion | flops 6289408 | bytes 6299648 | tf_op jit(solution)/shard_map/tkd,td->tk/dot_general | solution.py:558
  33.0 0.5 collective-permute-start.14
  33.5 0.8 copy-done.6
  34.3 1.4 collective-permute-start.10
  35.7 6.1 %collective-permute-done.2.refs_3_ = bf16[320,768]{1,0:T(8,128)(2,1)} collective-permute-done((bf16[320,768]{1,0:T(8,128)(2,1)}, bf16[320,768]{1,0:T(8,128)(2,1)}, u32[]{:S(2)}, u32[]{:S(2)}) %collective-permute-start.2) | collective-permute-done | bytes 491552 | tf_op jit(solution)/shard_map/ppermute | solution.py:537
  41.7 2.1 collective-permute-start.11
  43.8 0.0 collective-permute-done.3.refs_4_
  43.8 0.4 collective-permute-start.18
  44.3 20.0 %collective-permute-done.4.refs_5_ = bf16[320,768]{1,0:T(8,128)(2,1)} collective-permute-done((bf16[320,768]{1,0:T(8,128)(2,1)}, bf16[320,768]{1,0:T(8,128)(2,1)}, u32[]{:S(2)}, u32[]{:S(2)}) %collective-permute-start.4) | collective-permute-done | bytes 491552 | tf_op jit(solution)/shard_map/ppermute | solution.py:537
  64.2 0.4 collective-permute-start.17
  64.7 34.2 %own_rows.2 = (bf16[320,768]{1,0:T(8,128)(2,1)}, bf16[320,768]{1,0:T(8,128)(2,1)}, bf16[320,768]{1,0:T(8,128)(2,1)}, bf16[320,768]{1,0:T(8,128)(2,1)}, bf16[320,...) custom-call(s32[8]{0:T(128)} %get-tuple-element.40.rng_ref, ...), custom_call_target="tpu_custom_call" | custom-call | flops 16986931200 | bytes 50000000 | tf_op jit(solution)/shard_map/own_rows/pallas_call | solution.py:286
  98.9 0.0 collective-permute-done.10.refs_0_.refs_6_
  99.0 0.0 collective-permute-done.11.refs_1_.refs_7_
  99.0 0.8 copy-done.2
  99.7 9.9 %own_rows.3 = (bf16[320,768]{1,0:T(8,128)(2,1)}, bf16[320,768]{1,0:T(8,128)(2,1)}, bf16[3072,1536]{1,0:T(8,128)(2,1)}, bf16[3072,1536]{1,0:T(8,128)(2,1)}, bf16[3072,1536]{1,0:T(8,128)(2,1)}) custom-call(s32[8]{0:T(128)} %get-tuple-element.40.rng_ref, s32[52]{0:T(128)} %get-tuple-element.41.tl_ref, ...), custom_call_target="tpu_custom_call", output_to_operand_aliasing={{2}: (10, {}), {3}: (11, {}), {4}: (12, {})} | custom-call | flops 5662310400 | bytes 50000000 | tf_op jit(solution)/shard_map/own_rows/pallas_call | solution.py:286
  109.6 0.0 collective-permute-start.12
  109.7 9.2 %collective-permute-start.13 = (bf16[320,768]{1,0:T(8,128)(2,1)}, bf16[320,768]{1,0:T(8,128)(2,1)S(1)}, u32[]{:S(2)}, u32[]{:S(2)}) collective-permute-start(bf16[320,768]{1,0:T(8,128)(2,1)} %get-tuple-element.60), channel_id=1, source_target_pairs={{0,7},{1,6},{2,5},{3,4},{4,3},{5,2},{6,1},{7,0},{8,15},{9,14},{10,... | collective-permute-start | bytes 1474568 | tf_op jit(solution)/shard_map/ppermute | solution.py:556
  118.8 0.0 collective-permute-done.18.refs_0_
  118.9 13.6 %collective-permute-start.19 = (bf16[320,768]{1,0:T(8,128)(2,1)}, bf16[320,768]{1,0:T(8,128)(2,1)S(1)}, u32[]{:S(2)}, u32[]{:S(2)}) collective-permute-start(bf16[320,768]{1,0:T(8,128)(2,1)} %collective-permute-done.refs_1_), channel_id=1, source_target_pairs={{0,8},{8,0},{1,9},{9,1},{2,10},{10,2},{3,11},{11,3},{4,12},{12,4},... | collective-permute-start | bytes 1474568 | tf_op jit(solution)/shard_map/ppermute | solution.py:526
  132.4 1.1 broadcast_select_fusion.pos_ref
  133.5 1.9 plan.3
  135.5 26.9 %collective-permute-done.19.refs_1_ = bf16[320,768]{1,0:T(8,128)(2,1)S(1)} collective-permute-done((bf16[320,768]{1,0:T(8,128)(2,1)}, bf16[320,768]{1,0:T(8,128)(2,1)S(1)}, u32[]{:S(2)}, u32[]{:S(2)}) %collective-permute-start.19) | collective-permute-done | bytes 491552 | tf_op jit(solution)/shard_map/ppermute | solution.py:526
  162.3 1.5 collective-permute-start.6
  163.8 0.0 collective-permute-done.12.refs_6_
  163.8 0.0 collective-permute-start.7
  163.9 0.5 collective-permute-start.8
  164.4 1.4 collective-permute-start.9
  165.9 22.6 %own_dw.1 = (f32[768,1536]{1,0:T(8,128)}, f32[768,1536]{1,0:T(8,128)}, f32[1536,768]{1,0:T(8,128)}) custom-call(s32[8]{0:T(128)} %get-tuple-element.40.rng_ref, s32[52]{0:T(128)} %get-tuple-element.41.tl_ref, s32[2]{0:T(128)} %pad_add_fusion.meta_ref, bf16[320,768]{1,0:T(8,128)(2,1)} %get-tuple-element.42.refs_0_, ...), custom_call_target="tpu_custom_call" | custom-call | flops 11324620800 | bytes 50000000 | tf_op jit(solution)/shard_map/own_dw/pallas_call | solution.py:494
  188.4 0.0 collective-permute-done.6.refs_2_
  188.5 9.5 %collective-permute-start.20 = (bf16[320,768]{1,0:T(8,128)(2,1)S(1)}, bf16[320,768]{1,0:T(8,128)(2,1)S(1)}, u32[]{:S(2)}, u32[]{:S(2)}) collective-permute-start(bf16[320,768]{1,0:T(8,128)(2,1)S(1)} %copy-done.7), channel_id=1, source_target_pairs={{0,8},{8,0},{1,9},{9,1},{2,10},{10,2},{3,11},{11,3},{4,12},{12,4},... | collective-permute-start | bytes 1474568 | tf_op jit(solution)/shard_map/ppermute | solution.py:526
  198.0 0.1 collective-permute-start.21
  198.0 2.0 collective-permute-start.22
  200.0 0.0 collective-permute-done.9.refs_5_
  200.0 0.1 collective-permute-start.23
  200.1 13.1 %gather_rows.1 = bf16[2048,768]{1,0:T(8,128)(2,1)} custom-call(s32[2048,1]{1,0:T(8,128)} %broadcast_select_fusion.pos_ref, bf16[320,768]{1,0:T(8,128)(2,1)} %get-tuple-element.48.refs_0_, bf16[320,768]{1,0:T(8,128)(2,1)} %copy-done.11, bf16[320,768]{1,0:T(8,128)(2,1)} %copy-done.12, bf16[320,768]{1,0:T(8,128)(2,1)} %copy-done.14, ...), custom_call_target="tpu_custom_call" | custom-call | flops 8053063680 | bytes 7864320 | tf_op jit(solution)/shard_map/gather_rows/pallas_call | solution.py:107
  213.2 2.0 collective-permute-start.15
  215.2 5.5 %collective-permute-done.21.refs_3_ = bf16[320,768]{1,0:T(8,128)(2,1)} collective-permute-done((bf16[320,768]{1,0:T(8,128)(2,1)}, bf16[320,768]{1,0:T(8,128)(2,1)}, u32[]{:S(2)}, u32[]{:S(2)}) %collective-permute-start.21) | collective-permute-done | bytes 491552 | tf_op jit(solution)/shard_map/ppermute | solution.py:526
  220.7 2.0 collective-permute-start.16
  222.7 8.5 %collective-permute-done.22.refs_4_ = bf16[320,768]{1,0:T(8,128)(2,1)} collective-permute-done((bf16[320,768]{1,0:T(8,128)(2,1)}, bf16[320,768]{1,0:T(8,128)(2,1)}, u32[]{:S(2)}, u32[]{:S(2)}) %collective-permute-start.22) | collective-permute-done | bytes 491552 | tf_op jit(solution)/shard_map/ppermute | solution.py:526
  231.2 10.5 %collective-permute-done.23.refs_5_ = bf16[320,768]{1,0:T(8,128)(2,1)} collective-permute-done((bf16[320,768]{1,0:T(8,128)(2,1)}, bf16[320,768]{1,0:T(8,128)(2,1)}, u32[]{:S(2)}, u32[]{:S(2)}) %collective-permute-start.23) | collective-permute-done | bytes 491552 | tf_op jit(solution)/shard_map/ppermute | solution.py:526
  241.7 36.6 %peer_dw.2 = (f32[768,1536]{1,0:T(8,128)}, f32[768,1536]{1,0:T(8,128)}, f32[1536,768]{1,0:T(8,128)}) custom-call(s32[8]{0:T(128)} %get-tuple-element.61.rng_ref, s32[52]{0:T(128)} %get-tuple-element.62.tl_ref, s32[2]{0:T(128)} %pad_add_fusion.meta_ref, bf16[320,768]{1,0:T(8,128)(2,1)} %collective-permute-done.18.refs_0_, bf16[320,768]{1,0:T(8,128)(2,1)} %copy-done.8, ...), custom_call_target="tpu_custom_call" | custom-call | flops 16986931200 | bytes 50000000 | tf_op jit(solution)/shard_map/peer_dw/pallas_call | solution.py:494
  278.4 0.8 copy-done
  279.2 0.2 copy-done.1
  279.3 22.0 %peer_dw.3 = (f32[768,1536]{1,0:T(8,128)}, f32[768,1536]{1,0:T(8,128)}, f32[1536,768]{1,0:T(8,128)}) custom-call(s32[8]{0:T(128)} %get-tuple-element.61.rng_ref, s32[52]{0:T(128)} %get-tuple-element.62.tl_ref, s32[2]{0:T(128)} %pad_add_fusion.meta_ref, bf16[320,768]{1,0:T(8,128)(2,1)} %copy-done, bf16[320,768]{1,0:T(8,128)(2,1)} %copy-done.1, ...), custom_call_target="tpu_custom_call" | custom-call | flops 5662310400 | bytes 50000000 | tf_op jit(solution)/shard_map/peer_dw/pallas_call | solution.py:494
  (42 shorter events, 0.1 us)
Async XLA Ops:
  9.4 11.8 %copy-start.5 = (s32[2048,1]{0,1:T(1,128)S(1)}, s32[2048,1]{0,1:T(1,128)}, u32[]{:S(2)}) copy-start(s32[2048,1]{0,1:T(1,128)} %param.13) | copy-start | bytes 24580
  9.4 12.2 %copy-start.4 = (s32[2048,1]{0,1:T(1,128)S(1)}, s32[2048,1]{0,1:T(1,128)}, u32[]{:S(2)}) copy-start(s32[2048,1]{0,1:T(1,128)} %param.14) | copy-start | bytes 24580
  9.4 23.5 %collective-permute-start = (bf16[320,768]{1,0:T(8,128)(2,1)}, bf16[320,768]{1,0:T(8,128)(2,1)}, u32[]{:S(2)}, u32[]{:S(2)}) collective-permute-start(bf16[320,768]{1,0:T(8,128)(2,1)} %get-tuple-element.43), channel_id=1, source_target_pairs={{0,1},{1,0},{2,3},{3,2},{4,5},{5,4},{6,7},{7,6},{8,9},{9,8},{10,11... | collective-permute-start | bytes 1474568 | tf_op jit(solution)/shard_map/ppermute | solution.py:537
  17.7 15.8 %collective-permute-start.1 = (bf16[320,768]{1,0:T(8,128)(2,1)}, bf16[320,768]{1,0:T(8,128)(2,1)S(1)}, u32[]{:S(2)}, u32[]{:S(2)}) collective-permute-start(bf16[320,768]{1,0:T(8,128)(2,1)} %get-tuple-element.44), channel_id=1, source_target_pairs={{0,2},{1,3},{2,0},{3,1},{4,6},{5,7},{6,4},{7,5},{8,10},{9,11},{10,... | collective-permute-start | bytes 1474568 | tf_op jit(solution)/shard_map/ppermute | solution.py:537
  19.2 22.5 %collective-permute-start.2 = (bf16[320,768]{1,0:T(8,128)(2,1)}, bf16[320,768]{1,0:T(8,128)(2,1)}, u32[]{:S(2)}, u32[]{:S(2)}) collective-permute-start(bf16[320,768]{1,0:T(8,128)(2,1)} %get-tuple-element.45), channel_id=1, source_target_pairs={{0,3},{1,2},{2,1},{3,0},{4,7},{5,6},{6,5},{7,4},{8,11},{9,10},{10,... | collective-permute-start | bytes 1474568 | tf_op jit(solution)/shard_map/ppermute | solution.py:537
  19.6 24.3 %collective-permute-start.3 = (bf16[320,768]{1,0:T(8,128)(2,1)}, bf16[320,768]{1,0:T(8,128)(2,1)}, u32[]{:S(2)}, u32[]{:S(2)}) collective-permute-start(bf16[320,768]{1,0:T(8,128)(2,1)} %get-tuple-element.46), channel_id=1, source_target_pairs={{0,4},{1,5},{2,6},{3,7},{4,0},{5,1},{6,2},{7,3},{8,12},{9,13},{10,... | collective-permute-start | bytes 1474568 | tf_op jit(solution)/shard_map/ppermute | solution.py:537
  20.1 44.2 %collective-permute-start.4 = (bf16[320,768]{1,0:T(8,128)(2,1)}, bf16[320,768]{1,0:T(8,128)(2,1)}, u32[]{:S(2)}, u32[]{:S(2)}) collective-permute-start(bf16[320,768]{1,0:T(8,128)(2,1)} %get-tuple-element.47), channel_id=1, source_target_pairs={{0,5},{1,4},{2,7},{3,6},{4,1},{5,0},{6,3},{7,2},{8,13},{9,12},{10,... | collective-permute-start | bytes 1474568 | tf_op jit(solution)/shard_map/ppermute | solution.py:537
  25.5 7.5 %copy-start.15 = (s32[40]{0:T(128)S(1)}, s32[40]{0:T(128)}, u32[]{:S(2)}) copy-start(s32[40]{0:T(128)} %convert_element_type.3.occ_ref) | copy-start | bytes 484
  33.0 85.9 %collective-permute-start.14 = (s32[40]{0:T(128)S(1)}, s32[40]{0:T(128)S(1)}, u32[]{:S(2)}, u32[]{:S(2)}) collective-permute-start(s32[40]{0:T(128)S(1)} %copy-done.15), channel_id=1, source_target_pairs={{0,8},{8,0},{1,9},{9,1},{2,10},{10,2},{3,11},{11,3},{4,12},{12,4},... | collective-permute-start | bytes 488 | tf_op jit(solution)/shard_map/ppermute | solution.py:526
  33.5 0.8 copy-start.6
  34.3 64.7 %collective-permute-start.10 = (bf16[320,768]{1,0:T(8,128)(2,1)}, bf16[320,768]{1,0:T(8,128)(2,1)S(1)}, u32[]{:S(2)}, u32[]{:S(2)}) collective-permute-start(bf16[320,768]{1,0:T(8,128)(2,1)} %get-tuple-element.54), channel_id=1, source_target_pairs={{0,6},{1,7},{2,4},{3,5},{4,2},{5,3},{6,0},{7,1},{8,14},{9,15},{10,... | collective-permute-start | bytes 1474568 | tf_op jit(solution)/shard_map/ppermute | solution.py:537
  41.7 57.2 %collective-permute-start.11 = (bf16[320,768]{1,0:T(8,128)(2,1)}, bf16[320,768]{1,0:T(8,128)(2,1)}, u32[]{:S(2)}, u32[]{:S(2)}) collective-permute-start(bf16[320,768]{1,0:T(8,128)(2,1)} %get-tuple-element.55), channel_id=1, source_target_pairs={{0,7},{1,6},{2,5},{3,4},{4,3},{5,2},{6,1},{7,0},{8,15},{9,14},{10,... | collective-permute-start | bytes 1474568 | tf_op jit(solution)/shard_map/ppermute | solution.py:537
  43.8 75.0 %collective-permute-start.18 = (bf16[320,768]{1,0:T(8,128)(2,1)}, bf16[320,768]{1,0:T(8,128)(2,1)}, u32[]{:S(2)}, u32[]{:S(2)}) collective-permute-start(bf16[320,768]{1,0:T(8,128)(2,1)} %get-tuple-element.42.refs_0_), channel_id=1, source_target_pairs={{0,8},{8,0},{1,9},{9,1},{2,10},{10,2},{3,11},{11,3},{4,12},{12,4},... | collective-permute-start | bytes 1474568 | tf_op jit(solution)/shard_map/ppermute | solution.py:526
  64.2 177.5 %collective-permute-start.17 = (bf16[40,64,768]{2,1,0:T(8,128)(2,1)}, bf16[40,64,768]{2,1,0:T(8,128)(2,1)}, u32[]{:S(2)}, u32[]{:S(2)}) collective-permute-start(bf16[40,64,768]{2,1,0:T(8,128)(2,1)} %bitcast.12.refs_8_), channel_id=1, source_target_pairs={{0,8},{8,0},{1,9},{9,1},{2,10},{10,2},{3,11},{11,3},{4,12},{12,4},... | collective-permute-start | bytes 11796488 | tf_op jit(solution)/shard_map/ppermute | solution.py:526
  98.9 0.8 copy-start.2
  109.6 54.2 %collective-permute-start.12 = (bf16[320,768]{1,0:T(8,128)(2,1)}, bf16[320,768]{1,0:T(8,128)(2,1)S(1)}, u32[]{:S(2)}, u32[]{:S(2)}) collective-permute-start(bf16[320,768]{1,0:T(8,128)(2,1)} %get-tuple-element.59), channel_id=1, source_target_pairs={{0,6},{1,7},{2,4},{3,5},{4,2},{5,3},{6,0},{7,1},{8,14},{9,15},{10,... | collective-permute-start | bytes 1474568 | tf_op jit(solution)/shard_map/ppermute | solution.py:556
  109.7 54.2 %collective-permute-start.13 = (bf16[320,768]{1,0:T(8,128)(2,1)}, bf16[320,768]{1,0:T(8,128)(2,1)S(1)}, u32[]{:S(2)}, u32[]{:S(2)}) collective-permute-start(bf16[320,768]{1,0:T(8,128)(2,1)} %get-tuple-element.60), channel_id=1, source_target_pairs={{0,7},{1,6},{2,5},{3,4},{4,3},{5,2},{6,1},{7,0},{8,15},{9,14},{10,... | collective-permute-start | bytes 1474568 | tf_op jit(solution)/shard_map/ppermute | solution.py:556
  118.8 14.7 %copy-start.16 = (s32[40]{0:T(128)}, s32[40]{0:T(128)S(1)}, u32[]{:S(2)}) copy-start(s32[40]{0:T(128)S(1)} %collective-permute-done.14.occ_ref) | copy-start | bytes 484
  118.8 45.6 %collective-permute-start.5 = (bf16[320,768]{1,0:T(8,128)(2,1)}, bf16[320,768]{1,0:T(8,128)(2,1)S(1)}, u32[]{:S(2)}, u32[]{:S(2)}) collective-permute-start(bf16[320,768]{1,0:T(8,128)(2,1)} %get-tuple-element.49), channel_id=1, source_target_pairs={{0,1},{1,0},{2,3},{3,2},{4,5},{5,4},{6,7},{7,6},{8,9},{9,8},{10,11... | collective-permute-start | bytes 1474568 | tf_op jit(solution)/shard_map/ppermute | solution.py:553
  118.9 43.5 %collective-permute-start.19 = (bf16[320,768]{1,0:T(8,128)(2,1)}, bf16[320,768]{1,0:T(8,128)(2,1)S(1)}, u32[]{:S(2)}, u32[]{:S(2)}) collective-permute-start(bf16[320,768]{1,0:T(8,128)(2,1)} %collective-permute-done.refs_1_), channel_id=1, source_target_pairs={{0,8},{8,0},{1,9},{9,1},{2,10},{10,2},{3,11},{11,3},{4,12},{12,4},... | collective-permute-start | bytes 1474568 | tf_op jit(solution)/shard_map/ppermute | solution.py:526
  162.3 26.1 %copy-start.8 = (bf16[320,768]{1,0:T(8,128)(2,1)}, bf16[320,768]{1,0:T(8,128)(2,1)S(1)}, u32[]{:S(2)}) copy-start(bf16[320,768]{1,0:T(8,128)(2,1)S(1)} %collective-permute-done.19.refs_1_) | copy-start | bytes 1474564
  162.3 26.1 %collective-permute-start.6 = (bf16[320,768]{1,0:T(8,128)(2,1)}, bf16[320,768]{1,0:T(8,128)(2,1)S(1)}, u32[]{:S(2)}, u32[]{:S(2)}) collective-permute-start(bf16[320,768]{1,0:T(8,128)(2,1)} %get-tuple-element.50), channel_id=1, source_target_pairs={{0,2},{1,3},{2,0},{3,1},{4,6},{5,7},{6,4},{7,5},{8,10},{9,11},{10,... | collective-permute-start | bytes 1474568 | tf_op jit(solution)/shard_map/ppermute | solution.py:553
  163.8 2.0 copy-start.9
  163.8 34.1 %collective-permute-start.7 = (bf16[320,768]{1,0:T(8,128)(2,1)}, bf16[320,768]{1,0:T(8,128)(2,1)S(1)}, u32[]{:S(2)}, u32[]{:S(2)}) collective-permute-start(bf16[320,768]{1,0:T(8,128)(2,1)} %get-tuple-element.51), channel_id=1, source_target_pairs={{0,3},{1,2},{2,1},{3,0},{4,7},{5,6},{6,5},{7,4},{8,11},{9,10},{10,... | collective-permute-start | bytes 1474568 | tf_op jit(solution)/shard_map/ppermute | solution.py:553
  163.9 2.0 copy-start.10
  163.9 34.2 %collective-permute-start.8 = (bf16[320,768]{1,0:T(8,128)(2,1)}, bf16[320,768]{1,0:T(8,128)(2,1)}, u32[]{:S(2)}, u32[]{:S(2)}) collective-permute-start(bf16[320,768]{1,0:T(8,128)(2,1)} %get-tuple-element.52), channel_id=1, source_target_pairs={{0,4},{1,5},{2,6},{3,7},{4,0},{5,1},{6,2},{7,3},{8,12},{9,13},{10,... | collective-permute-start | bytes 1474568 | tf_op jit(solution)/shard_map/ppermute | solution.py:553
  164.4 1.4 copy-start.11
  164.4 35.6 %collective-permute-start.9 = (bf16[320,768]{1,0:T(8,128)(2,1)}, bf16[320,768]{1,0:T(8,128)(2,1)}, u32[]{:S(2)}, u32[]{:S(2)}) collective-permute-start(bf16[320,768]{1,0:T(8,128)(2,1)} %get-tuple-element.53), channel_id=1, source_target_pairs={{0,5},{1,4},{2,7},{3,6},{4,1},{5,0},{6,3},{7,2},{8,13},{9,12},{10,... | collective-permute-start | bytes 1474568 | tf_op jit(solution)/shard_map/ppermute | solution.py:553
  165.9 22.6 %copy-start.7 = (bf16[320,768]{1,0:T(8,128)(2,1)S(1)}, bf16[320,768]{1,0:T(8,128)(2,1)}, u32[]{:S(2)}) copy-start(bf16[320,768]{1,0:T(8,128)(2,1)} %copy-done.6) | copy-start | bytes 1474564
  188.5 11.6 %copy-start.12 = (bf16[320,768]{1,0:T(8,128)(2,1)}, bf16[320,768]{1,0:T(8,128)(2,1)S(1)}, u32[]{:S(2)}) copy-start(bf16[320,768]{1,0:T(8,128)(2,1)S(1)} %collective-permute-done.6.refs_2_) | copy-start | bytes 1474564
  188.5 24.7 %collective-permute-start.20 = (bf16[320,768]{1,0:T(8,128)(2,1)S(1)}, bf16[320,768]{1,0:T(8,128)(2,1)S(1)}, u32[]{:S(2)}, u32[]{:S(2)}) collective-permute-start(bf16[320,768]{1,0:T(8,128)(2,1)S(1)} %copy-done.7), channel_id=1, source_target_pairs={{0,8},{8,0},{1,9},{9,1},{2,10},{10,2},{3,11},{11,3},{4,12},{12,4},... | collective-permute-start | bytes 1474568 | tf_op jit(solution)/shard_map/ppermute | solution.py:526
  198.0 2.1 copy-start.14
  198.0 22.7 %collective-permute-start.21 = (bf16[320,768]{1,0:T(8,128)(2,1)}, bf16[320,768]{1,0:T(8,128)(2,1)}, u32[]{:S(2)}, u32[]{:S(2)}) collective-permute-start(bf16[320,768]{1,0:T(8,128)(2,1)} %collective-permute-done.2.refs_3_), channel_id=1, source_target_pairs={{0,8},{8,0},{1,9},{9,1},{2,10},{10,2},{3,11},{11,3},{4,12},{12,4},... | collective-permute-start | bytes 1474568 | tf_op jit(solution)/shard_map/ppermute | solution.py:526
  198.0 33.2 %collective-permute-start.22 = (bf16[320,768]{1,0:T(8,128)(2,1)}, bf16[320,768]{1,0:T(8,128)(2,1)}, u32[]{:S(2)}, u32[]{:S(2)}) collective-permute-start(bf16[320,768]{1,0:T(8,128)(2,1)} %collective-permute-done.3.refs_4_), channel_id=1, source_target_pairs={{0,8},{8,0},{1,9},{9,1},{2,10},{10,2},{3,11},{11,3},{4,12},{12,4},... | collective-permute-start | bytes 1474568 | tf_op jit(solution)/shard_map/ppermute | solution.py:526
  200.0 41.7 %collective-permute-start.23 = (bf16[320,768]{1,0:T(8,128)(2,1)}, bf16[320,768]{1,0:T(8,128)(2,1)}, u32[]{:S(2)}, u32[]{:S(2)}) collective-permute-start(bf16[320,768]{1,0:T(8,128)(2,1)} %collective-permute-done.4.refs_5_), channel_id=1, source_target_pairs={{0,8},{8,0},{1,9},{9,1},{2,10},{10,2},{3,11},{11,3},{4,12},{12,4},... | collective-permute-start | bytes 1474568 | tf_op jit(solution)/shard_map/ppermute | solution.py:526
  200.1 13.1 %copy-start.3 = (bf16[320,768]{1,0:T(8,128)(2,1)S(1)}, bf16[320,768]{1,0:T(8,128)(2,1)}, u32[]{:S(2)}) copy-start(bf16[320,768]{1,0:T(8,128)(2,1)} %copy-done.2) | copy-start | bytes 1474564
  213.2 28.5 %copy-start.13 = (bf16[320,768]{1,0:T(8,128)(2,1)}, bf16[320,768]{1,0:T(8,128)(2,1)S(1)}, u32[]{:S(2)}) copy-start(bf16[320,768]{1,0:T(8,128)(2,1)S(1)} %collective-permute-done.20.refs_2_) | copy-start | bytes 1474564
  213.2 65.2 %collective-permute-start.15 = (bf16[320,768]{1,0:T(8,128)(2,1)S(1)}, bf16[320,768]{1,0:T(8,128)(2,1)S(1)}, u32[]{:S(2)}, u32[]{:S(2)}) collective-permute-start(bf16[320,768]{1,0:T(8,128)(2,1)S(1)} %copy-done.3), channel_id=1, source_target_pairs={{0,8},{8,0},{1,9},{9,1},{2,10},{10,2},{3,11},{11,3},{4,12},{12,4},... | collective-permute-start | bytes 1474568 | tf_op jit(solution)/shard_map/ppermute | solution.py:526
  220.7 57.7 %collective-permute-start.16 = (bf16[320,768]{1,0:T(8,128)(2,1)}, bf16[320,768]{1,0:T(8,128)(2,1)S(1)}, u32[]{:S(2)}, u32[]{:S(2)}) collective-permute-start(bf16[320,768]{1,0:T(8,128)(2,1)} %collective-permute-done.11.refs_1_.refs_7_), channel_id=1, source_target_pairs={{0,8},{8,0},{1,9},{9,1},{2,10},{10,2},{3,11},{11,3},{4,12},{12,4},... | collective-permute-start | bytes 1474568 | tf_op jit(solution)/shard_map/ppermute | solution.py:526
  278.4 0.8 copy-start
  278.4 0.9 copy-start.1

commit v3 on v2

--- a/solution.py
+++ b/solution.py
@@ -130,9 +130,9 @@
         g_refs, refs = refs[:ng], refs[ng:]
         h1_ref, h3_ref, w1_hbm, w3_hbm, w2_hbm = refs[:5]
         refs = refs[5 + (3 if alias else 0):]
-        dxd_refs, refs = refs[:ng], refs[ng:]
+        dxd_refs, gcat_ref, refs = refs[:ng], refs[ng], refs[ng + 1:]
         (a_ref, dh1_ref, dh3_ref, w13v, w2v, gall, h1b, h3b, oall, hb, acc,
-         wsem, gsem, isem, osem, hsem) = refs
+         wsem, gsem, isem, osem, hsem, csem) = refs
         b0, b1 = rng_ref[at[0]], rng_ref[at[1]]
         half, me = meta_ref[0], meta_ref[1]
         c0 = half * (nc // 2)
@@ -196,6 +196,8 @@
         oall[...] = jnp.zeros(oall.shape, BF16)
         for c in gcopies:
             c.wait()
+        gcat = pltpu.make_async_copy(gall, gcat_ref, csem.at[0])
+        gcat.start()
 
         def weights(b, i, part):
             @pl.when(b == b0)
@@ -278,22 +280,23 @@
                     c.start()
                 for c in half_copies(b1):
                     c.wait()
+        gcat.wait()
         for c in outs:
             c.wait()
 
     hshape = jax.ShapeDtypeStruct((nblk * rows, fh), BF16)
     base = 3 + ng + 5
     return pl.pallas_call(
-        kernel, in_specs=[SMEM] * 3 + [HBM] * (ng + 5 + (3 if alias else 0)), out_specs=[HBM] * (ng + 3),
-        out_shape=[jax.ShapeDtypeStruct((cap, d), BF16)] * ng + [hshape] * 3,
-        input_output_aliases={base + q: ng + q for q in range(3)} if alias else {},
+        kernel, in_specs=[SMEM] * 3 + [HBM] * (ng + 5 + (3 if alias else 0)), out_specs=[HBM] * (ng + 4),
+        out_shape=[jax.ShapeDtypeStruct((cap, d), BF16)] * ng + [jax.ShapeDtypeStruct((ng * cap, d), BF16)] + [hshape] * 3,
+        input_output_aliases={base + q: ng + 1 + q for q in range(3)} if alias else {},
         scratch_shapes=[pltpu.VMEM((nc, d, 2 * fc), BF16), pltpu.VMEM((f, d), BF16),
                         pltpu.VMEM((ng * cap, d), BF16), pltpu.VMEM((2, rows, f), BF16), pltpu.VMEM((2, rows, f), BF16),
                         pltpu.VMEM((ng * cap, d), BF16), pltpu.VMEM((3, rows, fh), BF16),
                         pltpu.VMEM((rows, d), F32),
                         pltpu.SemaphoreType.DMA((nc, 3)), pltpu.SemaphoreType.DMA((ng,)),
                         pltpu.SemaphoreType.DMA((2, 2, BT)), pltpu.SemaphoreType.DMA((ng,)),
-                        pltpu.SemaphoreType.DMA((3,))],
+                        pltpu.SemaphoreType.DMA((3,)), pltpu.SemaphoreType.DMA((1,))],
         compiler_params=_params(), name="own_rows",
         cost_estimate=_cost(2 * 200 * ng * d * f * 3, 5e7),
     )(rng, tl, meta, *gs, h1, h3, w1, w3, w2, *(halves if alias else ()))
@@ -329,17 +332,17 @@
         name="plan", cost_estimate=_cost(1e6, 1e3))(occ, meta)
 
 
-def _dw(rng, tl, meta, first, gs, x, own, peer, sums, at, bt):
+def _dw(rng, tl, meta, first, gs, x, own, peer, sums, at, bt, tps):
     ng = len(gs)
-    cap, d = gs[0].shape
-    _, tile, _ = x.shape
-    tps = cap // tile
+    _, tile, d = x.shape
+    offs = [sum(g.shape[0] for g in gs[:q]) for q in range(ng + 1)]
+    gtiles = offs[ng] // tile
     fh = own[0].shape[1] if own else peer[0].shape[1] // 2
     rows = bt * tile
     fc = FC
     nc = fh // fc
     nadd = 3 if sums else 0
-    mb = -(-ng * tps // bt) + (1 if own else 0)
+    mb = -(-gtiles // bt) + (1 if own else 0)
 
     def kernel(rng_ref, tl_ref, meta_ref, *refs):
         g_refs, x_ref, refs = refs[:ng], refs[ng], refs[ng + 1:]
@@ -353,7 +356,8 @@
             t = lax.bitwise_xor(t // tps, me) * tps + lax.rem(t, tps)
             return pltpu.make_async_copy(x_ref.at[t], xb.at[b - b0, pl.ds(j * tile, tile)], xsem.at[b - b0, j])
 
-        gcopies = [pltpu.make_async_copy(g_refs[q], gall.at[pl.ds(q * cap, cap)], gsem.at[q]) for q in range(ng)]
+        gcopies = [pltpu.make_async_copy(g_refs[q], gall.at[pl.ds(offs[q], offs[q + 1] - offs[q])], gsem.at[q])
+                   for q in range(ng)]
 
         def pcopies(c, slot):
             cs = pl.ds(pl.multiple_of(c * fc, fc), fc)
@@ -405,8 +409,7 @@
         for c in gcopies:
             c.wait()
 
-        @pl.loop(b0, b1)
-        def _(b):
+        def ready(b):
             for j in range(bt):
                 @pl.when(tl_ref[b * bt + j] >= 0)
                 def _():
@@ -450,13 +453,19 @@
                     for cp in ocopies(c - 2, ps):
                         cp.wait()
 
-                p1[ps] = jnp.zeros((d, fc), F32)
-                p3[ps] = jnp.zeros((d, fc), F32)
-                p2[ps] = jnp.zeros((fc, d), F32)
+                @pl.when(b0 >= b1)
+                def _():
+                    for p in (p1, p3, p2):
+                        p[ps] = jnp.zeros(p.shape[1:], F32)
 
             @pl.loop(b0, b1)
             def _(b):
                 i = b - b0
+
+                @pl.when(c == 0)
+                def _():
+                    ready(b)
+
                 if own:
                     slot = lax.rem(c * (b1 - b0) + i, 2)
 
@@ -478,9 +487,10 @@
                     h3 = _dot(xb[i], sv[ps, 1]).astype(BF16)
                     da = _dot_nt(gb[i], sv[ps, 2])
                     a, dh1, dh3 = _grads(da, h1, h3)
-                p1[ps] += _dot(xt[i], dh1)
-                p3[ps] += _dot(xt[i], dh3)
-                p2[ps] += _dot(a.T, gb[i])
+                base = (lambda p: p[ps]) if sums else (lambda p: jnp.where(i > 0, p[ps], 0.0))
+                p1[ps] = base(p1) + _dot(xt[i], dh1)
+                p3[ps] = base(p3) + _dot(xt[i], dh3)
+                p2[ps] = base(p2) + _dot(a.T, gb[i])
 
             for cp in ocopies(c, ps):
                 cp.start()
@@ -493,13 +503,13 @@
     outs = [jax.ShapeDtypeStruct((d, fh), F32), jax.ShapeDtypeStruct((d, fh), F32), jax.ShapeDtypeStruct((fh, d), F32)]
     return pl.pallas_call(
         kernel, in_specs=[SMEM] * 3 + [HBM] * (ng + 4 + nadd), out_specs=[HBM] * 3, out_shape=outs,
-        scratch_shapes=[pltpu.VMEM((ng * cap, d), BF16), pltpu.VMEM((mb, rows, d), BF16), pltpu.VMEM((mb, d, rows), BF16),
+        scratch_shapes=[pltpu.VMEM((offs[ng], d), BF16), pltpu.VMEM((mb, rows, d), BF16), pltpu.VMEM((mb, d, rows), BF16),
                         pltpu.VMEM((mb, rows, d), BF16), pltpu.VMEM((2, 3, srows, fc), BF16),
                         pltpu.VMEM((2, d, fc), F32), pltpu.VMEM((2, d, fc), F32), pltpu.VMEM((2, fc, d), F32),
                         pltpu.SemaphoreType.DMA((ng,)), pltpu.SemaphoreType.DMA((mb, bt)),
                         pltpu.SemaphoreType.DMA((2, 3)), pltpu.SemaphoreType.DMA((2, 3)), pltpu.SemaphoreType.DMA((2, 3))],
         compiler_params=_params(), name="own_dw" if own else "peer_dw",
-        cost_estimate=_cost(2 * 200 * ng * d * fh * (3 if own else 6), 5e7),
+        cost_estimate=_cost(2 * 40 * gtiles * d * fh * (3 if own else 6), 5e7),
     )(rng, tl, meta, *gs, x, *(own or peer), *(sums or ()))
 
 
@@ -535,10 +545,6 @@
         dyd = [send[0]]
         for k in range(1, ne):
             dyd.append(lax.ppermute(send[k], 'expert', xor(k)))
-        dyo = []
-        for k in range(ne):
-            dyo.append(swap(dyd[k]))
-
         occ = jnp.any(x4 != 0, axis=(1, 2)).astype(I32)
         occo = swap(occ)
         nblk = -(-ka * tps // BT) + -(-(ne - ka) * tps // BT) + 1
@@ -547,19 +553,21 @@
 
         h14, h34 = h1.reshape(nt, TILE, f), h3.reshape(nt, TILE, f)
         wts = (w1[0], w3[0], w2[0])
-        *da, ha, hd1, hd3 = _own_rows(bnd, tl, meta, 0, dyd[:ka], h14, h34, *wts, None, nblk, (0, 1))
+        *da, ga, ha, hd1, hd3 = _own_rows(bnd, tl, meta, 0, dyd[:ka], h14, h34, *wts, None, nblk, (0, 1))
+        goa = swap(ga)
         back = [da[0]]
         for k in range(1, ka):
             back.append(lax.ppermute(da[k], 'expert', xor(k)))
-        *db, ha, hd1, hd3 = _own_rows(bnd, tl, meta, ka, dyd[ka:], h14, h34, *wts, (ha, hd1, hd3), nblk, (1, 2))
+        *db, gb, ha, hd1, hd3 = _own_rows(bnd, tl, meta, ka, dyd[ka:], h14, h34, *wts, (ha, hd1, hd3), nblk, (1, 2))
+        gob = swap(gb)
         for k in range(ka, ne):
             back.append(lax.ppermute(db[k - ka], 'expert', xor(k)))
-        sums = _dw(bnd, tl, meta, 0, dyd, x4, (ha, hd1, hd3), None, None, (0, 3), 2 * BT)
+        sums = _dw(bnd, tl, meta, 0, [ga, gb], x4, (ha, hd1, hd3), None, None, (0, 3), 2 * BT, tps)
         dg = jnp.einsum('tkd,td->tk', yd, dy, preferred_element_type=F32)
         cpos = jnp.where(slot >= 0, (topk_idx ^ me) * cap + slot, -1)
         dx = _gather_rows(cpos, back)
-        sums = _dw(bndo, tlo, meta, 0, dyo[:ka], xo, None, wts, sums, (0, 1), BT)
-        sums = _dw(bndo, tlo, meta, ka, dyo[ka:], xo, None, wts, sums, (1, 2), BT)
+        sums = _dw(bndo, tlo, meta, 0, [goa], xo, None, wts, sums, (0, 1), BT, tps)
+        sums = _dw(bndo, tlo, meta, ka, [gob], xo, None, wts, sums, (1, 2), BT, tps)
         dw1, dw3, dw2 = sums
         return dx, dg, dw1[None], dw3[None], dw2[None]
 

time: 302 us -> 268 us (0.89)
  waiting for transfers between devices: 77.4 us -> 55.7 us
  starting transfers between devices: 50.3 us -> 35.2 us
    ppermute x10 -> x4, waiting for transfers between devices: 51.4 us -> 0.01 us  [run(): swap = lambda v: lax.ppermute(v, 'data', zswap)]
    ppermute x2, waiting for transfers between devices: 0.01 us -> 13.8 us  [run(): back.append(lax.ppermute(db[k - ka], 'expert', xor(k)))]
    ppermute x5, waiting for transfers between devices: 0.01 us -> 9.49 us  [run(): back.append(lax.ppermute(da[k], 'expert', xor(k)))]
    ppermute x10 -> x4, starting transfers between devices: 30.5 us -> 23.2 us  [run(): swap = lambda v: lax.ppermute(v, 'data', zswap)]
    ppermute x7, waiting for transfers between devices: 26 us -> 32.3 us  [run(): dyd.append(lax.ppermute(send[k], 'expert', xor(k)))]
    ppermute x2, starting transfers between devices: 9.22 us -> 3.49 us  [run(): back.append(lax.ppermute(db[k - ka], 'expert', xor(k)))]
  transfers between devices with their start and end apart: 24 -> 18, of which waited for: 6 -> 6; matrix products, arithmetic and copies ran while one was open for 4% -> 4% of each run, Pallas kernels for 43% -> 49%
where the time goes in v3:
time: 268 us; the launch traced here: 267 us
  Pallas kernels  162 us (60%)
  waiting for transfers between devices  55.7 us (21%)
  starting transfers between devices  35.2 us (13%)
  other arithmetic  10 us (4%)
  local copies, waits for them, and re-layouts  3.53 us (1%)
    pallas_call x3, Pallas kernels, _dw(): pl.pallas_call(kernel, in_specs=[SMEM] * 3 + [HBM] * (ng + 4 + nadd), out...  83.2 us
    pallas_call x2, Pallas kernels, _own_rows(): pl.pallas_call(kernel, in_specs=[SMEM] * 3 + [HBM] * (ng + 5 + (3 if alia...  45.5 us
    ppermute x7, waiting for transfers between devices, run(): dyd.append(lax.ppermute(send[k], 'expert', xor(k)))  32.3 us
    ppermute x4, starting transfers between devices, run(): swap = lambda v: lax.ppermute(v, 'data', zswap)  23.2 us
    pallas_call x2, Pallas kernels, _scatter_rows(): pl.pallas_call(kernel, in_specs=[SMEM] + [vm] * 4, out_specs=[HBM] * k, o...  16.4 us
    ppermute x2, waiting for transfers between devices, run(): back.append(lax.ppermute(db[k - ka], 'expert', xor(k)))  13.8 us
    pallas_call x1, Pallas kernels, _gather_rows(): pl.pallas_call(kernel, grid=(t // tb,), in_specs=[pl.BlockSpec((tb, 1), l...  13 us
    ppermute x5, waiting for transfers between devices, run(): back.append(lax.ppermute(da[k], 'expert', xor(k)))  9.49 us
  transfers between devices with their start and end apart: 18, of which 6 were waited for; matrix products, arithmetic and copies ran while one was open for 4% of the time, Pallas kernels for 49%

profile of v3, /device:TPU:12, one launch (start us, length us, event | category | flops | bytes accessed | tf_op | source)
XLA Modules:
  0.0 267.5 jit_solution(11740111950769730331)
XLA Ops:
  0.6 0.7 pad_add_fusion.meta_ref
  1.3 8.2 %scatter_rows.2 = (bf16[320,768]{1,0:T(8,128)(2,1)}, bf16[320,768]{1,0:T(8,128)(2,1)}, bf16[320,768]{1,0:T(8,128)(2,1)}, bf16[320,768]{1,0:T(8,128)(2,1)}) custom-call(s32[2]{0:T(128)} %pad_add_fusion.meta_ref, s32[1,2048]{1,0:T(1,128)} %bitcast.37, s32[1,2048]{1,0:T(1,128)} %bitcast.35, f32[1,2048]{1,0:T(1,128)} %bitcast.43, bf16[2048,768]{1,0:T(8,128)(2,1)} %dy_ref.3), custom_call_target="tpu_custom_call" | custom-call | flops 4026531840 | bytes 3932160 | tf_op jit(solution)/shard_map/scatter_rows/pallas_call | solution.py:78
  9.5 0.0 copy-start.4
  9.5 0.0 collective-permute-start
  9.5 8.2 %scatter_rows.3 = (bf16[320,768]{1,0:T(8,128)(2,1)}, bf16[320,768]{1,0:T(8,128)(2,1)}, bf16[320,768]{1,0:T(8,128)(2,1)}, bf16[320,768]{1,0:T(8,128)(2,1)}) custom-call(s32[2]{0:T(128)} %pad_add_fusion.meta_ref, s32[1,2048]{1,0:T(1,128)} %bitcast.38, s32[1,2048]{1,0:T(1,128)} %bitcast.36, f32[1,2048]{1,0:T(1,128)} %bitcast.44, bf16[2048,768]{1,0:T(8,128)(2,1)} %dy_ref.3), custom_call_target="tpu_custom_call" | custom-call | flops 4026531840 | bytes 3932160 | tf_op jit(solution)/shard_map/scatter_rows/pallas_call | solution.py:78
  17.8 1.5 collective-permute-start.1
  19.3 0.4 collective-permute-start.2
  19.7 0.5 collective-permute-start.3
  20.2 1.1 collective-permute-start.4
  21.3 0.4 copy.29
  21.7 3.0 %compare_reduce_fusion = pred[2560]{0:T(1024)(128)(4,1)S(1)} fusion(bf16[1,2560,768]{2,1,0:T(8,128)(2,1)} %param.16), kind=kLoop, calls=%fused_computation | loop fusion | flops 3929600 | bytes 3934720 | tf_op jit(solution)/shard_map/reduce_or | solution.py:548
  24.7 0.1 reduce_or.14
  24.8 0.1 reduce_or.18
  25.0 0.6 convert_element_type.3.occ_ref
  25.5 1.9 plan.2
  27.4 0.1 xor_multiply_fusion
  27.5 0.0 collective-permute-done.refs_1_
  27.5 0.0 copy-start.8
  27.5 0.5 collective-permute-start.14
  28.0 4.1 %collective-permute-done.1.refs_2_ = bf16[320,768]{1,0:T(8,128)(2,1)S(1)} collective-permute-done((bf16[320,768]{1,0:T(8,128)(2,1)}, bf16[320,768]{1,0:T(8,128)(2,1)S(1)}, u32[]{:S(2)}, u32[]{:S(2)}) %collective-permute-start.1) | collective-permute-done | bytes 491552 | tf_op jit(solution)/shard_map/ppermute | solution.py:547
  32.1 1.4 collective-permute-start.10
  33.6 8.2 %collective-permute-done.2.refs_3_ = bf16[320,768]{1,0:T(8,128)(2,1)} collective-permute-done((bf16[320,768]{1,0:T(8,128)(2,1)}, bf16[320,768]{1,0:T(8,128)(2,1)}, u32[]{:S(2)}, u32[]{:S(2)}) %collective-permute-start.2) | collective-permute-done | bytes 491552 | tf_op jit(solution)/shard_map/ppermute | solution.py:547
  41.8 2.1 collective-permute-start.11
  43.9 0.0 collective-permute-done.3.refs_4_
  43.9 0.4 collective-permute-start.16
  44.4 20.0 %collective-permute-done.4.refs_5_ = bf16[320,768]{1,0:T(8,128)(2,1)} collective-permute-done((bf16[320,768]{1,0:T(8,128)(2,1)}, bf16[320,768]{1,0:T(8,128)(2,1)}, u32[]{:S(2)}, u32[]{:S(2)}) %collective-permute-start.4) | collective-permute-done | bytes 491552 | tf_op jit(solution)/shard_map/ppermute | solution.py:547
  64.3 35.2 %own_rows.2 = (bf16[320,768]{1,0:T(8,128)(2,1)}, bf16[320,768]{1,0:T(8,128)(2,1)}, bf16[320,768]{1,0:T(8,128)(2,1)}, bf16[320,768]{1,0:T(8,128)(2,1)}, bf16[320,...) custom-call(s32[8]{0:T(128)} %get-tuple-element.42.rng_ref, ...), custom_call_target="tpu_custom_call" | custom-call | flops 16986931200 | bytes 50000000 | tf_op jit(solution)/shard_map/own_rows/pallas_call | solution.py:289
  99.5 6.3 %collective-permute-start.17 = (bf16[1920,768]{1,0:T(8,128)(2,1)}, bf16[1920,768]{1,0:T(8,128)(2,1)}, u32[]{:S(2)}, u32[]{:S(2)}) collective-permute-start(bf16[1920,768]{1,0:T(8,128)(2,1)} %get-tuple-element.66.refs_0_), channel_id=1, source_target_pairs={{0,8},{8,0},{1,9},{9,1},{2,10},{10,2},{3,11},{11,3},{4,12},{12,4},... | collective-permute-start | bytes 8847368 | tf_op jit(solution)/shard_map/ppermute | solution.py:536
  105.8 0.0 collective-permute-done.10.refs_0_
  105.8 0.0 collective-permute-done.11.refs_1_
  105.8 0.0 copy-start.2
  105.8 0.8 copy-done.1
  106.6 0.2 copy-done.2
  106.8 10.3 %own_rows.3 = (bf16[320,768]{1,0:T(8,128)(2,1)}, bf16[320,768]{1,0:T(8,128)(2,1)}, bf16[640,768]{1,0:T(8,128)(2,1)}, bf16[3072,1536]{1,0:T(8,128)(2,1)}, bf16[30...) custom-call(s32[8]{0:T(128)} %get-tuple-element.42.rng_ref, ...), custom_call_target="tpu_custom_call", output_to_operand_aliasing={{3}: (10, {}), {4}: (11, {}), {5}: (12, {})} | custom-call | flops 5662310400 | bytes 50000000 | tf_op jit(solution)/shard_map/own_rows/pallas_call | solution.py:289
  117.0 0.0 copy-start.3
  117.1 0.0 collective-permute-start.12
  117.1 4.4 %fusion = f32[2048]{0:T(1024)} fusion(bf16[2048,768]{1,0:T(8,128)(2,1)} %dy_ref.3, bf16[2048,1,768]{2,0,1:T(8,128)(2,1)} %param.15), kind=kLoop, calls=%fused_computation.2 | loop fusion | flops 6289408 | bytes 6299648 | tf_op jit(solution)/shard_map/tkd,td->tk/dot_general | solution.py:566
  121.5 0.3 copy.31
  121.9 0.4 copy.33
  122.3 0.5 copy.32
  122.7 3.5 %collective-permute-start.13 = (bf16[320,768]{1,0:T(8,128)(2,1)}, bf16[320,768]{1,0:T(8,128)(2,1)S(1)}, u32[]{:S(2)}, u32[]{:S(2)}) collective-permute-start(bf16[320,768]{1,0:T(8,128)(2,1)} %get-tuple-element.62), channel_id=1, source_target_pairs={{0,7},{1,6},{2,5},{3,4},{4,3},{5,2},{6,1},{7,0},{8,15},{9,14},{10,... | collective-permute-start | bytes 1474568 | tf_op jit(solution)/shard_map/ppermute | solution.py:564
  126.2 0.0 collective-permute-done.14.occ_ref
  126.2 0.0 collective-permute-start.5
  126.2 5.8 %collective-permute-done.12.refs_6_ = bf16[320,768]{1,0:T(8,128)(2,1)S(1)} collective-permute-done((bf16[320,768]{1,0:T(8,128)(2,1)}, bf16[320,768]{1,0:T(8,128)(2,1)S(1)}, u32[]{:S(2)}, u32[]{:S(2)}) %collective-permute-start.12) | collective-permute-done | bytes 491552 | tf_op jit(solution)/shard_map/ppermute | solution.py:564
  132.0 0.0 collective-permute-start.6
  132.0 1.1 broadcast_select_fusion.pos_ref
  133.2 1.9 plan.3
  135.1 8.0 %collective-permute-done.13.refs_7_ = bf16[320,768]{1,0:T(8,128)(2,1)S(1)} collective-permute-done((bf16[320,768]{1,0:T(8,128)(2,1)}, bf16[320,768]{1,0:T(8,128)(2,1)S(1)}, u32[]{:S(2)}, u32[]{:S(2)}) %collective-permute-start.13) | collective-permute-done | bytes 491552 | tf_op jit(solution)/shard_map/ppermute | solution.py:564
  143.1 0.0 collective-permute-start.7
  143.1 0.0 collective-permute-done.5.refs_1_
  143.1 0.0 collective-permute-start.8
  143.2 9.5 %collective-permute-done.6.refs_2_ = bf16[320,768]{1,0:T(8,128)(2,1)} collective-permute-done((bf16[320,768]{1,0:T(8,128)(2,1)S(1)}, bf16[320,768]{1,0:T(8,128)(2,1)}, u32[]{:S(2)}, u32[]{:S(2)}) %collective-permute-start.6) | collective-permute-done | bytes 491552 | tf_op jit(solution)/shard_map/ppermute | solution.py:560
  152.7 1.4 collective-permute-start.9
  154.0 22.3 %own_dw.1 = (f32[768,1536]{1,0:T(8,128)}, f32[768,1536]{1,0:T(8,128)}, f32[1536,768]{1,0:T(8,128)}) custom-call(s32[8]{0:T(128)} %get-tuple-element.42.rng_ref, s32[52]{0:T(128)} %get-tuple-element.43.tl_ref, s32[2]{0:T(128)} %pad_add_fusion.meta_ref, bf16[1920,768]{1,0:T(8,128)(2,1)} %get-tuple-element.66.refs_0_, ...), custom_call_target="tpu_custom_call" | custom-call | flops 11324620800 | bytes 50000000 | tf_op jit(solution)/shard_map/own_dw/pallas_call | solution.py:504
  176.4 0.0 collective-permute-done.7.refs_3_
  176.4 16.0 %collective-permute-start.15 = (bf16[640,768]{1,0:T(8,128)(2,1)S(1)}, bf16[640,768]{1,0:T(8,128)(2,1)S(1)}, u32[]{:S(2)}, u32[]{:S(2)}) collective-permute-start(bf16[640,768]{1,0:T(8,128)(2,1)S(1)} %copy-done.5), channel_id=1, source_target_pairs={{0,8},{8,0},{1,9},{9,1},{2,10},{10,2},{3,11},{11,3},{4,12},{12,4},... | collective-permute-start | bytes 2949128 | tf_op jit(solution)/shard_map/ppermute | solution.py:536
  192.4 0.0 collective-permute-done.8.refs_4_
  192.4 0.0 collective-permute-done.9.refs_5_
  192.4 13.0 %gather_rows.1 = bf16[2048,768]{1,0:T(8,128)(2,1)} custom-call(s32[2048,1]{1,0:T(8,128)} %broadcast_select_fusion.pos_ref, bf16[320,768]{1,0:T(8,128)(2,1)} %get-tuple-element.50.refs_0_, bf16[320,768]{1,0:T(8,128)(2,1)} %collective-permute-done.5.refs_1_, bf16[320,768]{1,0:T(8,128)(2,1)} %collective-permute-done.6.refs_2_, ...), custom_call_target="tpu_custom_call" | custom-call | flops 8053063680 | bytes 7864320 | tf_op jit(solution)/shard_map/gather_rows/pallas_call | solution.py:107
  205.4 0.0 collective-permute-done.17.refs_0_
  205.4 0.0 collective-permute-done.16.refs_1_
  205.4 38.1 %peer_dw.2 = (f32[768,1536]{1,0:T(8,128)}, f32[768,1536]{1,0:T(8,128)}, f32[1536,768]{1,0:T(8,128)}) custom-call(s32[8]{0:T(128)} %get-tuple-element.63.rng_ref, s32[52]{0:T(128)} %get-tuple-element.64.tl_ref, s32[2]{0:T(128)} %pad_add_fusion.meta_ref, bf16[1920,768]{1,0:T(8,128)(2,1)} %collective-permute-done.17.refs_0_, ...), custom_call_target="tpu_custom_call" | custom-call | flops 16986931200 | bytes 50000000 | tf_op jit(solution)/shard_map/peer_dw/pallas_call | solution.py:504
  243.6 0.9 copy-done
  244.5 22.8 %peer_dw.3 = (f32[768,1536]{1,0:T(8,128)}, f32[768,1536]{1,0:T(8,128)}, f32[1536,768]{1,0:T(8,128)}) custom-call(s32[8]{0:T(128)} %get-tuple-element.63.rng_ref, s32[52]{0:T(128)} %get-tuple-element.64.tl_ref, s32[2]{0:T(128)} %pad_add_fusion.meta_ref, bf16[640,768]{1,0:T(8,128)(2,1)} %copy-done, bf16[40,64,768]{2,1,0:T(8,128)(2,1)} %collective-permute-done.16.refs_1_, ...), custom_call_target="tpu_custom_call" | custom-call | flops 5662310400 | bytes 50000000 | tf_op jit(solution)/shard_map/peer_dw/pallas_call | solution.py:504
  (20 shorter events, 0.1 us)
Async XLA Ops:
  9.5 11.8 %copy-start.4 = (s32[2048,1]{0,1:T(1,128)S(1)}, s32[2048,1]{0,1:T(1,128)}, u32[]{:S(2)}) copy-start(s32[2048,1]{0,1:T(1,128)} %param.13) | copy-start | bytes 24580
  9.5 18.0 %collective-permute-start = (bf16[320,768]{1,0:T(8,128)(2,1)}, bf16[320,768]{1,0:T(8,128)(2,1)S(1)}, u32[]{:S(2)}, u32[]{:S(2)}) collective-permute-start(bf16[320,768]{1,0:T(8,128)(2,1)} %get-tuple-element.45), channel_id=1, source_target_pairs={{0,1},{1,0},{2,3},{3,2},{4,5},{5,4},{6,7},{7,6},{8,9},{9,8},{10,11... | collective-permute-start | bytes 1474568 | tf_op jit(solution)/shard_map/ppermute | solution.py:547
  17.8 14.3 %collective-permute-start.1 = (bf16[320,768]{1,0:T(8,128)(2,1)}, bf16[320,768]{1,0:T(8,128)(2,1)S(1)}, u32[]{:S(2)}, u32[]{:S(2)}) collective-permute-start(bf16[320,768]{1,0:T(8,128)(2,1)} %get-tuple-element.46), channel_id=1, source_target_pairs={{0,2},{1,3},{2,0},{3,1},{4,6},{5,7},{6,4},{7,5},{8,10},{9,11},{10,... | collective-permute-start | bytes 1474568 | tf_op jit(solution)/shard_map/ppermute | solution.py:547
  19.3 22.5 %collective-permute-start.2 = (bf16[320,768]{1,0:T(8,128)(2,1)}, bf16[320,768]{1,0:T(8,128)(2,1)}, u32[]{:S(2)}, u32[]{:S(2)}) collective-permute-start(bf16[320,768]{1,0:T(8,128)(2,1)} %get-tuple-element.47), channel_id=1, source_target_pairs={{0,3},{1,2},{2,1},{3,0},{4,7},{5,6},{6,5},{7,4},{8,11},{9,10},{10,... | collective-permute-start | bytes 1474568 | tf_op jit(solution)/shard_map/ppermute | solution.py:547
  19.7 24.3 %collective-permute-start.3 = (bf16[320,768]{1,0:T(8,128)(2,1)}, bf16[320,768]{1,0:T(8,128)(2,1)}, u32[]{:S(2)}, u32[]{:S(2)}) collective-permute-start(bf16[320,768]{1,0:T(8,128)(2,1)} %get-tuple-element.48), channel_id=1, source_target_pairs={{0,4},{1,5},{2,6},{3,7},{4,0},{5,1},{6,2},{7,3},{8,12},{9,13},{10,... | collective-permute-start | bytes 1474568 | tf_op jit(solution)/shard_map/ppermute | solution.py:547
  20.2 44.2 %collective-permute-start.4 = (bf16[320,768]{1,0:T(8,128)(2,1)}, bf16[320,768]{1,0:T(8,128)(2,1)}, u32[]{:S(2)}, u32[]{:S(2)}) collective-permute-start(bf16[320,768]{1,0:T(8,128)(2,1)} %get-tuple-element.49), channel_id=1, source_target_pairs={{0,5},{1,4},{2,7},{3,6},{4,1},{5,0},{6,3},{7,2},{8,13},{9,12},{10,... | collective-permute-start | bytes 1474568 | tf_op jit(solution)/shard_map/ppermute | solution.py:547
  27.5 4.6 %copy-start.8 = (bf16[320,768]{1,0:T(8,128)(2,1)}, bf16[320,768]{1,0:T(8,128)(2,1)S(1)}, u32[]{:S(2)}) copy-start(bf16[320,768]{1,0:T(8,128)(2,1)S(1)} %collective-permute-done.refs_1_) | copy-start | bytes 1474564
  27.5 98.7 %collective-permute-start.14 = (s32[40]{0:T(128)}, s32[40]{0:T(128)}, u32[]{:S(2)}, u32[]{:S(2)}) collective-permute-start(s32[40]{0:T(128)} %convert_element_type.3.occ_ref), channel_id=1, source_target_pairs={{0,8},{8,0},{1,9},{9,1},{2,10},{10,2},{3,11},{11,3},{4,12},{12,4},... | collective-permute-start | bytes 488 | tf_op jit(solution)/shard_map/ppermute | solution.py:536
  32.1 9.7 %copy-start.10 = (bf16[320,768]{1,0:T(8,128)(2,1)}, bf16[320,768]{1,0:T(8,128)(2,1)S(1)}, u32[]{:S(2)}) copy-start(bf16[320,768]{1,0:T(8,128)(2,1)S(1)} %collective-permute-done.1.refs_2_) | copy-start | bytes 1474564
  32.1 73.7 %collective-permute-start.10 = (bf16[320,768]{1,0:T(8,128)(2,1)}, bf16[320,768]{1,0:T(8,128)(2,1)S(1)}, u32[]{:S(2)}, u32[]{:S(2)}) collective-permute-start(bf16[320,768]{1,0:T(8,128)(2,1)} %get-tuple-element.56), channel_id=1, source_target_pairs={{0,6},{1,7},{2,4},{3,5},{4,2},{5,3},{6,0},{7,1},{8,14},{9,15},{10,... | collective-permute-start | bytes 1474568 | tf_op jit(solution)/shard_map/ppermute | solution.py:547
  41.8 64.0 %collective-permute-start.11 = (bf16[320,768]{1,0:T(8,128)(2,1)}, bf16[320,768]{1,0:T(8,128)(2,1)S(1)}, u32[]{:S(2)}, u32[]{:S(2)}) collective-permute-start(bf16[320,768]{1,0:T(8,128)(2,1)} %get-tuple-element.57), channel_id=1, source_target_pairs={{0,7},{1,6},{2,5},{3,4},{4,3},{5,2},{6,1},{7,0},{8,15},{9,14},{10,... | collective-permute-start | bytes 1474568 | tf_op jit(solution)/shard_map/ppermute | solution.py:547
  43.9 161.5 %collective-permute-start.16 = (bf16[40,64,768]{2,1,0:T(8,128)(2,1)}, bf16[40,64,768]{2,1,0:T(8,128)(2,1)}, u32[]{:S(2)}, u32[]{:S(2)}) collective-permute-start(bf16[40,64,768]{2,1,0:T(8,128)(2,1)} %bitcast.33), channel_id=1, source_target_pairs={{0,8},{8,0},{1,9},{9,1},{2,10},{10,2},{3,11},{11,3},{4,12},{12,4},... | collective-permute-start | bytes 11796488 | tf_op jit(solution)/shard_map/ppermute | solution.py:536
  99.5 105.9 %collective-permute-start.17 = (bf16[1920,768]{1,0:T(8,128)(2,1)}, bf16[1920,768]{1,0:T(8,128)(2,1)}, u32[]{:S(2)}, u32[]{:S(2)}) collective-permute-start(bf16[1920,768]{1,0:T(8,128)(2,1)} %get-tuple-element.66.refs_0_), channel_id=1, source_target_pairs={{0,8},{8,0},{1,9},{9,1},{2,10},{10,2},{3,11},{11,3},{4,12},{12,4},... | collective-permute-start | bytes 8847368 | tf_op jit(solution)/shard_map/ppermute | solution.py:536
  105.8 0.8 copy-start.1
  105.8 0.9 copy-start.2
  117.0 4.8 %copy-start.3 = (s32[2048,1]{0,1:T(1,128)S(1)}, s32[2048,1]{0,1:T(1,128)}, u32[]{:S(2)}) copy-start(s32[2048,1]{0,1:T(1,128)} %param.14) | copy-start | bytes 24580
  117.0 9.2 %copy-start.9 = (bf16[320,768]{1,0:T(8,128)(2,1)S(1)}, bf16[320,768]{1,0:T(8,128)(2,1)}, u32[]{:S(2)}) copy-start(bf16[320,768]{1,0:T(8,128)(2,1)} %get-tuple-element.51) | copy-start | bytes 1474564
  117.0 15.0 %copy-start.6 = (bf16[320,768]{1,0:T(8,128)(2,1)S(1)}, bf16[320,768]{1,0:T(8,128)(2,1)}, u32[]{:S(2)}) copy-start(bf16[320,768]{1,0:T(8,128)(2,1)} %get-tuple-element.52) | copy-start | bytes 1474564
  117.1 15.0 %collective-permute-start.12 = (bf16[320,768]{1,0:T(8,128)(2,1)}, bf16[320,768]{1,0:T(8,128)(2,1)S(1)}, u32[]{:S(2)}, u32[]{:S(2)}) collective-permute-start(bf16[320,768]{1,0:T(8,128)(2,1)} %get-tuple-element.61), channel_id=1, source_target_pairs={{0,6},{1,7},{2,4},{3,5},{4,2},{5,3},{6,0},{7,1},{8,14},{9,15},{10,... | collective-permute-start | bytes 1474568 | tf_op jit(solution)/shard_map/ppermute | solution.py:564
  122.7 20.4 %collective-permute-start.13 = (bf16[320,768]{1,0:T(8,128)(2,1)}, bf16[320,768]{1,0:T(8,128)(2,1)S(1)}, u32[]{:S(2)}, u32[]{:S(2)}) collective-permute-start(bf16[320,768]{1,0:T(8,128)(2,1)} %get-tuple-element.62), channel_id=1, source_target_pairs={{0,7},{1,6},{2,5},{3,4},{4,3},{5,2},{6,1},{7,0},{8,15},{9,14},{10,... | collective-permute-start | bytes 1474568 | tf_op jit(solution)/shard_map/ppermute | solution.py:564
  126.2 16.9 %collective-permute-start.5 = (bf16[320,768]{1,0:T(8,128)(2,1)S(1)}, bf16[320,768]{1,0:T(8,128)(2,1)}, u32[]{:S(2)}, u32[]{:S(2)}) collective-permute-start(bf16[320,768]{1,0:T(8,128)(2,1)S(1)} %copy-done.9), channel_id=1, source_target_pairs={{0,1},{1,0},{2,3},{3,2},{4,5},{5,4},{6,7},{7,6},{8,9},{9,8},{10,11... | collective-permute-start | bytes 1474568 | tf_op jit(solution)/shard_map/ppermute | solution.py:560
  132.0 22.0 %copy-start.7 = (bf16[320,768]{1,0:T(8,128)(2,1)}, bf16[320,768]{1,0:T(8,128)(2,1)S(1)}, u32[]{:S(2)}) copy-start(bf16[320,768]{1,0:T(8,128)(2,1)S(1)} %collective-permute-done.12.refs_6_) | copy-start | bytes 1474564
  132.0 20.6 %collective-permute-start.6 = (bf16[320,768]{1,0:T(8,128)(2,1)S(1)}, bf16[320,768]{1,0:T(8,128)(2,1)}, u32[]{:S(2)}, u32[]{:S(2)}) collective-permute-start(bf16[320,768]{1,0:T(8,128)(2,1)S(1)} %copy-done.6), channel_id=1, source_target_pairs={{0,2},{1,3},{2,0},{3,1},{4,6},{5,7},{6,4},{7,5},{8,10},{9,11},{10,... | collective-permute-start | bytes 1474568 | tf_op jit(solution)/shard_map/ppermute | solution.py:560
  143.1 10.9 %copy-start.11 = (bf16[320,768]{1,0:T(8,128)(2,1)}, bf16[320,768]{1,0:T(8,128)(2,1)S(1)}, u32[]{:S(2)}) copy-start(bf16[320,768]{1,0:T(8,128)(2,1)S(1)} %collective-permute-done.13.refs_7_) | copy-start | bytes 1474564
  143.1 33.3 %collective-permute-start.7 = (bf16[320,768]{1,0:T(8,128)(2,1)}, bf16[320,768]{1,0:T(8,128)(2,1)}, u32[]{:S(2)}, u32[]{:S(2)}) collective-permute-start(bf16[320,768]{1,0:T(8,128)(2,1)} %get-tuple-element.53), channel_id=1, source_target_pairs={{0,3},{1,2},{2,1},{3,0},{4,7},{5,6},{6,5},{7,4},{8,11},{9,10},{10,... | collective-permute-start | bytes 1474568 | tf_op jit(solution)/shard_map/ppermute | solution.py:560
  143.1 49.2 %collective-permute-start.8 = (bf16[320,768]{1,0:T(8,128)(2,1)}, bf16[320,768]{1,0:T(8,128)(2,1)}, u32[]{:S(2)}, u32[]{:S(2)}) collective-permute-start(bf16[320,768]{1,0:T(8,128)(2,1)} %get-tuple-element.54), channel_id=1, source_target_pairs={{0,4},{1,5},{2,6},{3,7},{4,0},{5,1},{6,2},{7,3},{8,12},{9,13},{10,... | collective-permute-start | bytes 1474568 | tf_op jit(solution)/shard_map/ppermute | solution.py:560
  152.7 39.7 %collective-permute-start.9 = (bf16[320,768]{1,0:T(8,128)(2,1)}, bf16[320,768]{1,0:T(8,128)(2,1)}, u32[]{:S(2)}, u32[]{:S(2)}) collective-permute-start(bf16[320,768]{1,0:T(8,128)(2,1)} %get-tuple-element.55), channel_id=1, source_target_pairs={{0,5},{1,4},{2,7},{3,6},{4,1},{5,0},{6,3},{7,2},{8,13},{9,12},{10,... | collective-permute-start | bytes 1474568 | tf_op jit(solution)/shard_map/ppermute | solution.py:560
  154.0 22.4 %copy-start.5 = (bf16[640,768]{1,0:T(8,128)(2,1)S(1)}, bf16[640,768]{1,0:T(8,128)(2,1)}, u32[]{:S(2)}) copy-start(bf16[640,768]{1,0:T(8,128)(2,1)} %get-tuple-element.65.refs_1_) | copy-start | bytes 2949124
  176.4 67.2 %collective-permute-start.15 = (bf16[640,768]{1,0:T(8,128)(2,1)S(1)}, bf16[640,768]{1,0:T(8,128)(2,1)S(1)}, u32[]{:S(2)}, u32[]{:S(2)}) collective-permute-start(bf16[640,768]{1,0:T(8,128)(2,1)S(1)} %copy-done.5), channel_id=1, source_target_pairs={{0,8},{8,0},{1,9},{9,1},{2,10},{10,2},{3,11},{11,3},{4,12},{12,4},... | collective-permute-start | bytes 2949128 | tf_op jit(solution)/shard_map/ppermute | solution.py:536
  243.6 0.9 copy-start
